TPU v7x, 32 devices: a whole 2x2x4 slice. The times are simulated.
32 devices in a mesh: sfc: 8 (over z, x), grp: 4 (over y, core).
Axes of the slice: x: 2, y: 2, z: 4, core: 2. Of those that a mesh axis runs over, the one named last changes fastest.
Arguments:
- source: float32 [32, 16, 1024], P('sfc', None, 'grp'), may hold values from -8 to 8
- layer_counts: int32 [8], P('sfc'), may hold values from 1 to 4, 21 in all
Outputs:
- solution: float32 [32, 16, 1024], P('sfc', None, 'grp')
- residual: float32 [32, 16, 1024], P('sfc', None, 'grp')
- direction: float32 [32, 16, 1024], P('sfc', None, 'grp')
Inputs may be any that keep to these rules, and one draw needn't show every extreme that they name: `layer_counts`: each entry counts the live leading slots of that index of sfc; they sum to 21, and at least one entry equals 4.
All inputs are finite; a program needn't handle non-finite values. No bound on the sum of `layer_counts` on one device may be relied on, other than what follows from the above.
Results may differ from a plain program's by a relative error of at most 0.00011.
Values sent between devices are 32-bit elements; how exact they have to be, the bound alone decides.
A program may use at most 64 MiB of HBM per device.

v0:
```python
import functools

import jax
import jax.numpy as jnp
from jax import lax
from jax.experimental import pallas as pl
from jax.experimental.pallas import tpu as pltpu
from jax.sharding import PartitionSpec as P

MESH = pl.DeviceIdType.MESH
OMEGA = 2.0 / 3.0
LANES = 128
SUBS = 8
COARSE_SWEEPS = 4
POST_SWEEPS = 2
WAYS = ((0, 1), (0, -1), (1, 0), (1, 1), (1, -1), (-1, 0), (-1, 1), (-1, -1))


def kernel(
    dims, count_hbm, source_hbm, first_ref, image_ref, w_ref, source_out, scale_ref,
    source_ref, image_buf, counts, rhs, smooth, other, coarse, ea, eb, mask, own, packed,
    side, below, above, part, red, local_sem,
    send_sem, recv_sem, red_send, red_recv, hello,
):
    slots, edge, tiles, n_sfc, n_grp = dims
    planes = slots * edge
    sfc = lax.axis_index("sfc")
    grp = lax.axis_index("grp")
    me = sfc * n_grp + grp
    everyone = n_sfc * n_grp
    step = OMEGA / 6.0
    cstep = OMEGA / 1.5
    middle = (SUBS - tiles) // 2

    def there(ds, dg):
        flag = None
        if ds:
            flag = sfc < n_sfc - 1 if ds > 0 else sfc > 0
        if dg:
            extra = grp < n_grp - 1 if dg > 0 else grp > 0
            flag = extra if flag is None else jnp.logical_and(flag, extra)
        return flag

    gossip = n_sfc <= 9 and n_grp <= 4
    barrier = pltpu.get_barrier_semaphore()

    def place(i):
        peer = lax.rem(me + i, everyone)
        return peer, {"sfc": peer // n_grp, "grp": lax.rem(peer, n_grp)}

    def greet(i, carry):
        pl.semaphore_signal(barrier, inc=1, device_id=place(i)[1], device_id_type=MESH)
        return carry

    count_copy = pltpu.make_async_copy(count_hbm, counts, local_sem.at[0])
    source_copy = pltpu.make_async_copy(source_hbm, source_ref, local_sem.at[1])
    count_copy.start()
    source_copy.start()
    if gossip:
        for ds, dg in WAYS:
            @pl.when(there(ds, dg))
            def _(ds=ds, dg=dg):
                pl.semaphore_signal(
                    barrier, inc=1, device_id={"sfc": sfc + ds, "grp": grp + dg},
                    device_id_type=MESH,
                )
    else:
        lax.fori_loop(1, everyone, greet, 0)

    def one(flag):
        return jnp.where(flag, 1, 0)

    def greet_far(rnd, far):
        if gossip and far < n_sfc:
            for ds in (far, -far):
                @pl.when(sfc + ds < n_sfc if ds > 0 else sfc + ds >= 0)
                def _(ds=ds):
                    pl.semaphore_signal(
                        hello.at[rnd], inc=1, device_id={"sfc": sfc + ds}, device_id_type=MESH
                    )

    def hear_far(rnd, far):
        if gossip and far < n_sfc:
            pl.semaphore_wait(hello.at[rnd], one(sfc + far < n_sfc) + one(sfc >= far))

    lane = lax.broadcasted_iota(jnp.int32, (1, SUBS, LANES), 2)
    sub = lax.broadcasted_iota(jnp.int32, (1, SUBS, LANES), 1)
    z = lane % edge

    def has(flag_int):
        return flag_int > 0

    has_below = one(sfc > 0)
    has_above = one(sfc < n_sfc - 1)
    has_left = one(grp > 0)
    has_right = one(grp < n_grp - 1)
    owned = jnp.logical_and(sub >= middle, sub < middle + tiles)
    lefts = jnp.logical_and(sub >= middle - tiles, sub < middle)
    rights = jnp.logical_and(sub >= middle + tiles, sub < middle + 2 * tiles)
    rows_ok = (
        jnp.where(owned, 1, 0) + jnp.where(lefts, 1, 0) * has_left
        + jnp.where(rights, 1, 0) * has_right
    )
    def zero_rhs(i, carry):
        rhs[pl.ds(i * SUBS, SUBS), :] = jnp.zeros((SUBS, LANES), jnp.float32)
        return carry

    lax.fori_loop(0, planes + 2 * edge + 2, zero_rhs, 0)

    count_copy.wait()
    count = counts[0]
    for s in range(slots + 2):
        if s == 0:
            ok = has_below
        else:
            ok = one(count >= s) + one(count == s - 1) * has_above
        mask[pl.ds(SUBS * s, SUBS), :] = (rows_ok * ok).astype(jnp.float32)[0]

    for s in range(slots):
        mine = jnp.where(owned, 1, 0) * one(count > s)
        own[pl.ds(SUBS * s, SUBS), :] = mine.astype(jnp.float32)[0]

    def copies(e, i, ds, dg, src):
        gpos = 1 - dg
        if ds == 0:
            source, target = src, side.at[e, gpos // 2]
        else:
            tile, amount = ((0, 2), (1, 3), (3, 2))[dg + 1]
            source = packed.at[e, int(ds > 0), pl.ds(tile, amount)]
            target = (below if ds > 0 else above).at[e, gpos, pl.ds(0, amount)]
        return pltpu.make_async_remote_copy(
            src_ref=source, dst_ref=target, send_sem=send_sem.at[e, i],
            recv_sem=recv_sem.at[e, i], device_id={"sfc": sfc + ds, "grp": grp + dg},
            device_id_type=MESH,
        )

    def start(e, src):
        for i, (ds, dg) in enumerate(WAYS):
            @pl.when(there(ds, dg))
            def _(i=i, ds=ds, dg=dg):
                copies(e, i, ds, dg, src).start()

    def receive(e, src):
        for i, (ds, dg) in enumerate(WAYS):
            @pl.when(there(-ds, -dg))
            def _(i=i, ds=ds, dg=dg):
                copies(e, i, ds, dg, src).wait_recv()

    def sent(e, src):
        for i, (ds, dg) in enumerate(WAYS):
            @pl.when(there(ds, dg))
            def _(i=i, ds=ds, dg=dg):
                copies(e, i, ds, dg, src).wait_send()

    def pack(e, src):
        cut = SUBS // 2
        for up in (0, 1):
            rows = pl.ds(0, edge)
            value = [src[rows, pl.ds(t * LANES, LANES)] for t in range(tiles)]
            if up:
                for s in range(1, slots):
                    rows = pl.ds(s * edge, edge)
                    value = [
                        jnp.where(count > s, src[rows, pl.ds(t * LANES, LANES)], value[t])
                        for t in range(tiles)
                    ]
            if up:
                near = [v[edge - SUBS :] for v in value]
                far = [v[edge - SUBS - cut : edge - SUBS] for v in value]
                edges = [v[edge - cut :] for v in value]
            else:
                near = [v[:SUBS] for v in value]
                far = [v[SUBS : SUBS + cut] for v in value]
                edges = [v[:cut] for v in value]
            packed[e, up, 0] = jnp.concatenate([far[0], edges[1]], axis=0)
            packed[e, up, 1] = near[0]
            packed[e, up, 2] = jnp.concatenate([far[0], far[1]], axis=0)
            packed[e, up, 3] = near[1]
            packed[e, up, 4] = jnp.concatenate([far[1], edges[0]], axis=0)

    def ghost(ref, e, up, g, h, t):
        cut = SUBS // 2
        near_h = 1 if up else 0
        if g == 1:
            if h == near_h:
                return ref[e, g, 0 if t == 0 else 2]
            mix, low = ref[e, g, 1], t == 0
        else:
            full = 1 if g == 0 else 0
            if h == near_h and t == full:
                return ref[e, g, 0 if g == 0 else 1]
            mix = ref[e, g, 1 if g == 0 else 0]
            if h == near_h:
                low = False
            elif t == full:
                low = True
            else:
                return jnp.zeros((SUBS, LANES), jnp.float32)
        half = mix[:cut] if low else mix[cut:]
        none = jnp.zeros((cut, LANES), jnp.float32)
        return jnp.concatenate([none, half] if up else [half, none], axis=0)

    def unpack(e, src):
        sides = ((0, has_left), (1, 1), (2, has_right))
        for g, present in sides:
            for s in range(slots + 2):
                for h in range(edge // SUBS):
                    for t in range(tiles):
                        cols = pl.ds(t * LANES, LANES)
                        rows = pl.ds(h * SUBS, SUBS)

                        def centre(slot):
                            at = pl.ds(slot * edge + h * SUBS, SUBS)
                            return src[at, cols] if g == 1 else side[e, g // 2, at, cols]

                        if s == 0:
                            value = jnp.where(has(has_below * present), ghost(below, e, 1, g, h, t), 0.0)
                        else:
                            up = one(count == s - 1) * has_above * present
                            value = jnp.zeros((SUBS, LANES), jnp.float32)
                            if s >= 2:
                                value = jnp.where(has(up), ghost(above, e, 0, g, h, t), value)
                            if s <= slots:
                                value = jnp.where(has(one(count >= s) * present), centre(s - 1), value)
                        plane = 1 + s * edge + h * SUBS
                        at_sub = middle + (g - 1) * tiles + t
                        rhs[pl.ds(plane * SUBS + at_sub, SUBS, stride=SUBS), :] = value

    def roll(v, amount, axis):
        return pltpu.roll(v, amount % v.shape[axis], axis)

    def inplane(v, dz, dy):
        up_z = jnp.where(z < edge - dz, roll(v, -dz, 2), 0.0)
        down_z = jnp.where(z >= dz, roll(v, dz, 2), 0.0)
        ru = roll(v, -dy, 2)
        up_y = jnp.where(lane < LANES - dy, ru, roll(ru, -1, 1))
        rd = roll(v, dy, 2)
        down_y = jnp.where(lane >= dy, rd, roll(rd, 1, 1))
        return (up_z + down_z) + (up_y + down_y)

    def load(ref, p, n):
        return ref[pl.ds((p + 1) * SUBS, n * SUBS), :].reshape(n, SUBS, LANES)

    def store(ref, p, value):
        n = value.shape[0]
        ref[pl.ds((p + 1) * SUBS, n * SUBS), :] = value.reshape(n * SUBS, LANES)

    def lap(ref, p, n, dz=1, dy=edge):
        wide = load(ref, p - 1, n + 2)
        v = wide[1:-1]
        return v, 6.0 * v - (wide[:-2] + wide[2:]) - inplane(v, dz, dy)

    def slot_mask(s):
        return mask[pl.ds(SUBS * s, SUBS), :][None]

    chunk = SUBS
    per_slot = edge // chunk
    chunks = (slots + 2) * per_slot

    def vcycle(on_sum=None):
        acc = jnp.zeros((SUBS, LANES), jnp.float32)
        for c in range(chunks):
            r, applied = lap(rhs, c * chunk, chunk)
            store(smooth, c * chunk, slot_mask(c // per_slot) * (2.0 * step * r - step * step * applied))
        for c in range(chunks):
            v, applied = lap(smooth, c * chunk, chunk)
            r = load(rhs, c * chunk, chunk)
            q = r - applied
            s = c // per_slot - 1
            if on_sum is not None and 0 <= s < slots:
                acc = acc + own[pl.ds(SUBS * s, SUBS), :] * jnp.sum((r + q) * v, axis=0)
            q = q.reshape(chunk // 2, 2, SUBS, LANES)
            q = q[:, 0] + q[:, 1]
            q = q + jnp.where(lane % 2 == 0, roll(q, -1, 2), roll(q, 1, 2))
            q = q + jnp.where(lane // edge % 2 == 0, roll(q, -edge, 2), roll(q, edge, 2))
            store(coarse, c * chunk // 2, slot_mask(c // per_slot) * (0.125 * q))
        half = edge // 2
        for s in range(slots + 2):
            v, applied = lap(coarse, s * half, half, 2, 2 * edge)
            store(ea, s * half, slot_mask(s) * (2.0 * cstep * v - 0.25 * cstep * cstep * applied))
        now, then = ea, eb
        for sweep in range(COARSE_SWEEPS - 2):
            for s in range(slots + 2):
                v, applied = lap(now, s * half, half, 2, 2 * edge)
                c = load(coarse, s * half, half)
                value = slot_mask(s) * (v + cstep * (c - 0.25 * applied))
                store(then, s * half, value)
            now, then = then, now
        if on_sum is not None:
            for s in range(slots):
                ce = load(coarse, (s + 1) * half, half) * load(now, (s + 1) * half, half)
                acc = acc + own[pl.ds(SUBS * s, SUBS), :] * (2.0 * jnp.sum(ce, axis=0))
            on_sum(acc)
        for c in range(1, chunks - 1):
            e = load(now, c * chunk // 2, chunk // 2)[:, None]
            e = jnp.broadcast_to(e, (chunk // 2, 2, SUBS, LANES)).reshape(chunk, SUBS, LANES)
            store(smooth, c * chunk, load(smooth, c * chunk, chunk) + e)
        now, then = smooth, other
        for sweep in range(POST_SWEEPS):
            for c in range(1, chunks - 1):
                v, applied = lap(now, c * chunk, chunk)
                r = load(rhs, c * chunk, chunk)
                store(then, c * chunk, slot_mask(c // per_slot) * (v + step * (r - applied)))
            now, then = then, now
        return now

    def natural(ref, s, h, t):
        plane = 1 + (s + 1) * edge + h * SUBS
        return ref[pl.ds(plane * SUBS + middle + t, SUBS, stride=SUBS), :]

    def owned_tiles():
        for s in range(slots):
            for h in range(edge // SUBS):
                for t in range(tiles):
                    yield s, h, t, pl.ds(s * edge + h * SUBS, SUBS), pl.ds(t * LANES, LANES)

    source_copy.wait()
    pack(0, source_ref)
    if gossip:
        near = (1 + one(sfc > 0) + one(sfc < n_sfc - 1)) * (1 + one(grp > 0) + one(grp < n_grp - 1))
        pl.semaphore_wait(barrier, near - 1)
    else:
        pl.semaphore_wait(barrier, everyone - 1)
    start(0, source_ref)
    receive(0, source_ref)
    greet_far(0, 2)
    unpack(0, source_ref)
    z0 = vcycle()
    for c in range(per_slot, chunks - per_slot):
        _, applied = lap(z0, c * chunk, chunk)
        store(other, c * chunk, applied)
    acc_rz = jnp.zeros((SUBS, LANES), jnp.float32)
    acc_curv = jnp.zeros((SUBS, LANES), jnp.float32)
    for s, h, t, rows, cols in owned_tiles():
        value = natural(z0, s, h, t)
        image = natural(other, s, h, t)
        source = source_ref[rows, cols]
        if s:
            value = jnp.where(count > s, value, 0.0)
            image = jnp.where(count > s, image, 0.0)
            source = jnp.where(count > s, source, 0.0)
        first_ref[rows, cols] = value
        image_ref[rows, cols] = image
        image_buf[rows, cols] = image
        source_out[rows, cols] = source
        acc_rz = acc_rz + source * value
        acc_curv = acc_curv + value * image
    pack(1, image_buf)
    hear_far(0, 2)
    start(1, image_buf)
    row = lax.broadcasted_iota(jnp.int32, (1, LANES), 1)

    def whole(acc):
        return jnp.sum(jnp.sum(acc, axis=0, keepdims=True), axis=1, keepdims=True)

    rz, curv = whole(acc_rz), whole(acc_curv)
    known = jnp.where(row == 0, rz, jnp.where(row == 1, curv, 0.0))
    receive(1, image_buf)
    greet_far(1, 4)
    unpack(1, image_buf)

    def send(slot, peer, device):
        return pltpu.make_async_remote_copy(
            src_ref=part, dst_ref=red.at[slot], send_sem=red_send.at[peer],
            recv_sem=red_recv.at[slot], device_id=device, device_id_type=MESH,
        )

    def spread(acc):
        value = jnp.where(row == 2, whole(acc), known)
        part[...] = value
        red[me] = value
        hear_far(1, 4)

        def go(i, carry):
            peer, device = place(i)
            send(me, peer, device).start()
            return carry

        lax.fori_loop(1, everyone, go, 0)

    w = vcycle(spread)
    for s, h, t, rows, cols in owned_tiles():
        value = natural(w, s, h, t)
        if s:
            value = jnp.where(count > s, value, 0.0)
        w_ref[rows, cols] = value
    sent(0, source_ref)
    sent(1, image_buf)

    def got(i, carry):
        peer, device = place(i)
        send(peer, peer, device).wait_recv()
        return carry

    lax.fori_loop(1, everyone, got, 0)
    sums = jnp.sum(red[...], axis=0)

    def pick(i):
        return jnp.sum(jnp.where(row == i, sums, 0.0), axis=1, keepdims=True)

    alpha = pick(0) / pick(1)
    ratio = pick(2) / pick(1)
    scale_ref[...] = jnp.concatenate(
        [jnp.broadcast_to(alpha, (1, LANES)), jnp.broadcast_to(ratio, (1, LANES))], axis=0
    )

    def out(i, carry):
        peer, device = place(i)
        send(me, peer, device).wait_send()
        return carry

    lax.fori_loop(1, everyone, out, 0)


def combine(first, image, w, source, scale, solution_ref, residual_ref, direction_ref):
    alpha = scale[0:1, 0:1]
    ratio = scale[1:2, 0:1]
    solution_ref[...] = alpha * first[...]
    residual_ref[...] = source[...] - alpha * image[...]
    direction_ref[...] = alpha * (ratio * first[...] - w[...])


def shards(n_sfc, n_grp, source, layer_counts):
    slots, edge, width = source.shape
    planes, tiles = slots * edge, width // LANES
    padded = (planes + 2 * edge + 2) * SUBS
    half_padded = ((slots + 2) * edge // 2 + 2) * SUBS
    f32 = jnp.float32
    vmem = pltpu.VMEM
    dma = pltpu.SemaphoreType.DMA
    n = n_sfc * n_grp
    out = jax.ShapeDtypeStruct((planes, width), f32)
    parts = pl.pallas_call(
        functools.partial(kernel, (slots, edge, tiles, n_sfc, n_grp)),
        out_shape=(out, out, out, out, jax.ShapeDtypeStruct((2, LANES), f32)),
        in_specs=[pl.BlockSpec(memory_space=pl.ANY)] * 2,
        out_specs=[pl.BlockSpec(memory_space=pltpu.VMEM)] * 5,
        scratch_shapes=[
            vmem((planes, width), f32),
            vmem((planes, width), f32),
            pltpu.SMEM((1,), jnp.int32),
            vmem((padded, LANES), f32),
            vmem((padded, LANES), f32),
            vmem((padded, LANES), f32),
            vmem((half_padded, LANES), f32),
            vmem((half_padded, LANES), f32),
            vmem((half_padded, LANES), f32),
            vmem(((slots + 2) * SUBS, LANES), f32),
            vmem((slots * SUBS, LANES), f32),
            vmem((2, 2, 5, SUBS, LANES), f32),
            vmem((2, 2, planes, width), f32),
            vmem((2, 3, 3, SUBS, LANES), f32),
            vmem((2, 3, 3, SUBS, LANES), f32),
            vmem((1, LANES), f32),
            vmem((n, 1, LANES), f32),
            dma((2,)),
            dma((2, len(WAYS))),
            dma((2, len(WAYS))),
            dma((n,)),
            dma((n,)),
            pltpu.SemaphoreType.REGULAR((2,)),
        ],
        compiler_params=pltpu.CompilerParams(
            collective_id=0, has_side_effects=True, vmem_limit_bytes=16 * 1024 * 1024
        ),
        name="pcg",
    )(layer_counts, source.reshape(planes, width))
    outs = pl.pallas_call(
        combine,
        out_shape=(out, out, out),
        in_specs=[pl.BlockSpec(memory_space=pltpu.VMEM)] * 5,
        out_specs=[pl.BlockSpec(memory_space=pltpu.VMEM)] * 3,
        compiler_params=pltpu.CompilerParams(vmem_limit_bytes=16 * 1024 * 1024),
        name="combine",
    )(*parts)
    return tuple(o.reshape(source.shape) for o in outs)


def solution(mesh):
    n_sfc, n_grp = mesh.shape["sfc"], mesh.shape["grp"]
    return jax.shard_map(
        functools.partial(shards, n_sfc, n_grp),
        mesh=mesh,
        in_specs=(P("sfc", None, "grp"), P("sfc")),
        out_specs=(P("sfc", None, "grp"), P("sfc", None, "grp"), P("sfc", None, "grp")),
        check_vma=False,
    )
```

profile of v0, /device:TPU:0, one launch (start us, length us, event | category | flops | bytes accessed | tf_op | source)
XLA Modules:
  0.0 28.0 jit_solution(15638111848480014852)
XLA Ops:
  1.3 0.0 copy-start
  1.3 0.8 %copy-done = f32[4,16,256]{2,1,0:T(8,128)S(1)} copy-done((f32[4,16,256]{2,1,0:T(8,128)S(1)}, f32[4,16,256]{2,1,0:T(8,128)}, u32[]{:S(2)}) %copy-start) | copy-done | bytes 65560
  2.1 25.1 %pcg.1 = (f32[64,256]{1,0:T(8,128)S(1)}, f32[64,256]{1,0:T(8,128)S(1)}, f32[64,256]{1,0:T(8,128)S(1)}, f32[64,256]{1,0:T(8,128)S(1)}, f32[2,128]{1,0:T(2,128)S(1)}) custom-call(s32[1]{0:T(128)S(6)} %copy.5.count_hbm, f32[64,256]{1,0:T(8,128)S(1)} %bitcast.4), custom_call_target="tpu_custom_call" | custom-call | tf_op jit(solution)/shard_map/pcg/pallas_call | solution.py:433
  27.2 0.7 %combine.1 = (f32[64,256]{1,0:T(8,128)}, f32[64,256]{1,0:T(8,128)}, f32[64,256]{1,0:T(8,128)}) custom-call(f32[64,256]{1,0:T(8,128)S(1)} %get-tuple-element.11.first, f32[64,256]{1,0:T(8,128)S(1)} %get-tuple-element.12.image, f32[64,256]{1,0:T(8,128)S(1)} %get-tuple-element.13.w, f32[64,256]{1,0:T(8,128)S(1)} %get-tuple-element.14.source, ...), custom_call_target="tpu_custom_call" | custom-call | tf_op jit(solution)/shard_map/combine/pallas_call | solution.py:468
Async XLA Ops:
  1.3 0.8 %copy-start = (f32[4,16,256]{2,1,0:T(8,128)S(1)}, f32[4,16,256]{2,1,0:T(8,128)}, u32[]{:S(2)}) copy-start(f32[4,16,256]{2,1,0:T(8,128)} %param.2) | copy-start | bytes 196612
where the time goes:
time: 28.1 us; the launch traced here: 28 us
  Pallas kernels  25.8 us (92%)
  between operations  1.29 us (5%)
  local copies, waits for them, and re-layouts  0.83 us (3%)
    pallas_call x1, Pallas kernels, shards(): pl.pallas_call(functools.partial(kernel, (slots, edge, tiles, n_sfc, n_gr...  25.1 us
    unnamed x2, local copies, waits for them, and re-layouts  0.83 us
    pallas_call x1, Pallas kernels, shards(): pl.pallas_call(combine, out_shape=(out, out, out), in_specs=[pl.BlockSpec...  0.72 us

commit v1 on v0

v1 whole, which is shorter than its diff:
```python
import functools

import jax
import jax.numpy as jnp
import numpy as np
from jax import lax
from jax.experimental import pallas as pl
from jax.experimental.pallas import tpu as pltpu
from jax.sharding import PartitionSpec as P

MESH = pl.DeviceIdType.MESH
LANES = 128
SUBS = 8
STEP = 1.0 / 9.0
CSTEP = 4.0 / 9.0
WAYS = ((0, 1), (0, -1), (1, 0), (1, 1), (1, -1), (-1, 0), (-1, 1), (-1, -1))


def weights(edge):
    lane = np.arange(LANES)
    y, z = lane // edge, lane % edge

    def parts(y, z, last):
        dy, dz = y[None, :] - y[:, None], z[None, :] - z[:, None]
        one = 3.0 * ((dy == 0) & (dz == 0)) + ((dy == 0) & (abs(dz) == 1)) + ((abs(dy) == 1) & (dz == 0))
        down = 1.0 * ((dy == last) & (dz == 0))
        up = 1.0 * ((dy == -last) & (dz == 0))
        return one, down, up

    one, down, up = parts(y, z, SUBS - 1)
    two = one @ one + down @ up + up @ down
    side = down + up
    fine = [2 * one, 2 * side, two, one @ side + side @ one]
    one, down, up = parts(y // 2, z // 2, SUBS // 2 - 1)
    same = 1.0 * ((y[None, :] // 2 == y[:, None] // 2) & (z[None, :] // 2 == z[:, None] // 2))
    two = (one @ one + down @ up + up @ down) / 4
    down2, up2 = (one @ down + down @ one) / 4, (one @ up + up @ one) / 4
    three = (two @ one + down2 @ up + up2 @ down) / 4
    down3, up3 = (two @ down + down2 @ one) / 4, (two @ up + up2 @ one) / 4
    coarse = [same, one, two, three, down + up, down2 + up2, down3, up3]
    whole = np.concatenate(fine + coarse, axis=1)
    return whole.astype(jnp.bfloat16)


def split(x, pieces):
    out = []
    for i in range(pieces):
        part = x.astype(jnp.bfloat16)
        out.append(part)
        if i < pieces - 1:
            x = x - part.astype(jnp.float32)
    return out


def kernel(
    dims, count_hbm, source_hbm, weight_hbm, first_ref, image_ref, w_ref, source_out, scale_ref,
    source_ref, image_buf, counts, fine_w, coarse_w, rhs, pre, gather, other, coarse, ea, eb,
    mask, cmask, own, packed, side, below, above, part, red, local_sem,
    send_sem, recv_sem, red_sem, hello,
):
    slots, edge, tiles, n_sfc, n_grp = dims
    half = edge // 2
    planes = slots * edge
    rows, crows = (slots + 2) * edge, (slots + 2) * half
    wide = 3 * tiles
    mids = tuple(range(tiles - 1, 2 * tiles + 1))
    mine = tuple(range(tiles, 2 * tiles))
    f32 = jnp.float32
    sfc = lax.axis_index("sfc")
    grp = lax.axis_index("grp")
    me = sfc * n_grp + grp
    everyone = n_sfc * n_grp

    def there(ds, dg):
        flag = None
        if ds:
            flag = sfc < n_sfc - 1 if ds > 0 else sfc > 0
        if dg:
            extra = grp < n_grp - 1 if dg > 0 else grp > 0
            flag = extra if flag is None else jnp.logical_and(flag, extra)
        return flag

    gossip = n_sfc <= 9 and n_grp <= 4
    barrier = pltpu.get_barrier_semaphore()

    def place(i):
        peer = lax.rem(me + i, everyone)
        return peer, {"sfc": peer // n_grp, "grp": lax.rem(peer, n_grp)}

    def greet(i, carry):
        pl.semaphore_signal(barrier, inc=1, device_id=place(i)[1], device_id_type=MESH)
        return carry

    source_copy = pltpu.make_async_copy(source_hbm, source_ref, local_sem.at[1])
    count_copy = pltpu.make_async_copy(count_hbm, counts, local_sem.at[0])
    source_copy.start()
    count_copy.start()
    weight_copies = []
    for i, (ref, at, width) in enumerate(((fine_w, 0, 4 * LANES), (coarse_w, 4 * LANES, 8 * LANES))):
        for up in (0, 1):
            copy = pltpu.make_async_copy(
                weight_hbm.at[:, pl.ds(at, width)], ref.at[pl.ds(up * LANES, LANES), :],
                local_sem.at[2 + 2 * i + up],
            )
            copy.start()
            weight_copies.append(copy)
    if gossip:
        for ds, dg in WAYS:
            @pl.when(there(ds, dg))
            def _(ds=ds, dg=dg):
                pl.semaphore_signal(
                    barrier, inc=1, device_id={"sfc": sfc + ds, "grp": grp + dg},
                    device_id_type=MESH,
                )
    else:
        lax.fori_loop(1, everyone, greet, 0)

    def one(flag):
        return jnp.where(flag, 1, 0)

    def greet_far(rnd, far):
        if gossip and far < n_sfc:
            for ds in (far, -far):
                @pl.when(sfc + ds < n_sfc if ds > 0 else sfc + ds >= 0)
                def _(ds=ds):
                    pl.semaphore_signal(
                        hello.at[rnd], inc=1, device_id={"sfc": sfc + ds}, device_id_type=MESH
                    )

    def hear_far(rnd, far):
        if gossip and far < n_sfc:
            pl.semaphore_wait(hello.at[rnd], one(sfc + far < n_sfc) + one(sfc >= far))

    lane = lax.broadcasted_iota(jnp.int32, (SUBS, LANES), 1)
    low_half = lane < LANES // 2

    def has(flag_int):
        return flag_int > 0

    has_below = one(sfc > 0)
    has_above = one(sfc < n_sfc - 1)
    has_left = one(grp > 0)
    has_right = one(grp < n_grp - 1)

    zero = jnp.zeros((SUBS, LANES), f32)
    for ref in (rhs, pre, gather, other):
        for t in range(wide):
            ref[t, pl.ds(0, SUBS), :] = zero
            ref[t, pl.ds(SUBS + rows, SUBS), :] = zero
    for t in range(wide):
        for ref in (coarse, ea, eb):
            ref[t, pl.ds(0, SUBS), :] = zero
            ref[t, pl.ds(SUBS + crows, SUBS), :] = zero
    for t in range(wide):
        for at in (SUBS, rows):
            other[t, pl.ds(at, SUBS), :] = zero

    source_copy.wait()

    def copies(e, i, ds, dg, src):
        gpos = 1 - dg
        if ds == 0:
            source, target = src, side.at[e, gpos // 2]
        else:
            tile, amount = ((0, 2), (1, 3), (3, 2))[dg + 1]
            source = packed.at[e, int(ds > 0), pl.ds(tile, amount)]
            target = (below if ds > 0 else above).at[e, gpos, pl.ds(0, amount)]
        return pltpu.make_async_remote_copy(
            src_ref=source, dst_ref=target, send_sem=send_sem.at[i],
            recv_sem=recv_sem.at[e, i], device_id={"sfc": sfc + ds, "grp": grp + dg},
            device_id_type=MESH,
        )

    def start(e, src):
        for i, (ds, dg) in enumerate(WAYS):
            @pl.when(there(ds, dg))
            def _(i=i, ds=ds, dg=dg):
                copies(e, i, ds, dg, src).start()

    def receive(e, src):
        for i, (ds, dg) in enumerate(WAYS):
            @pl.when(there(-ds, -dg))
            def _(i=i, ds=ds, dg=dg):
                copies(e, i, ds, dg, src).wait_recv()

    def sent(e, src):
        for i, (ds, dg) in enumerate(WAYS):
            @pl.when(there(ds, dg))
            def _(i=i, ds=ds, dg=dg):
                copies(e, i, ds, dg, src).wait_send()

    def pack(e, src):
        cut = SUBS // 2
        for up in (0, 1):
            at = pl.ds(0, edge)
            value = [src[at, pl.ds(t * LANES, LANES)] for t in range(tiles)]
            if up:
                for s in range(1, slots):
                    at = pl.ds(s * edge, edge)
                    value = [
                        jnp.where(count > s, src[at, pl.ds(t * LANES, LANES)], value[t])
                        for t in range(tiles)
                    ]
            if up:
                near = [v[edge - SUBS :] for v in value]
                far = [v[edge - SUBS - cut : edge - SUBS] for v in value]
                edges = [v[edge - cut :] for v in value]
            else:
                near = [v[:SUBS] for v in value]
                far = [v[SUBS : SUBS + cut] for v in value]
                edges = [v[:cut] for v in value]
            packed[e, up, 0] = jnp.concatenate([far[0], edges[1]], axis=0)
            packed[e, up, 1] = near[0]
            packed[e, up, 2] = jnp.concatenate([far[0], far[1]], axis=0)
            packed[e, up, 3] = near[1]
            packed[e, up, 4] = jnp.concatenate([far[1], edges[0]], axis=0)

    def ghost(ref, e, up, g, h, t):
        cut = SUBS // 2
        near_h = 1 if up else 0
        if g == 1:
            if h == near_h:
                return ref[e, g, 0 if t == 0 else 2]
            mix, low = ref[e, g, 1], t == 0
        else:
            full = 1 if g == 0 else 0
            if h == near_h and t == full:
                return ref[e, g, 0 if g == 0 else 1]
            mix = ref[e, g, 1 if g == 0 else 0]
            if h == near_h:
                low = False
            elif t == full:
                low = True
            else:
                return jnp.zeros((SUBS, LANES), f32)
        part = mix[:cut] if low else mix[cut:]
        none = jnp.zeros((cut, LANES), f32)
        return jnp.concatenate([none, part] if up else [part, none], axis=0)

    def unpack(e, src):
        sides = ((0, has_left), (1, 1), (2, has_right))
        for g, present in sides:
            for s in range(slots + 2):
                for h in range(edge // SUBS):
                    for t in range(tiles):
                        cols = pl.ds(t * LANES, LANES)

                        def centre(slot):
                            at = pl.ds(slot * edge + h * SUBS, SUBS)
                            return src[at, cols] if g == 1 else side[e, g // 2, at, cols]

                        if s == 0:
                            value = jnp.where(has(has_below * present), ghost(below, e, 1, g, h, t), 0.0)
                        else:
                            up = one(count == s - 1) * has_above * present
                            value = jnp.zeros((SUBS, LANES), f32)
                            if s >= 2:
                                value = jnp.where(has(up), ghost(above, e, 0, g, h, t), value)
                            if s <= slots:
                                value = jnp.where(has(one(count >= s) * present), centre(s - 1), value)
                        rhs[g * tiles + t, pl.ds(SUBS + s * edge + h * SUBS, SUBS), :] = value

    def body(ref, t, first=0, n=rows):
        return ref[t, pl.ds(SUBS + first, n), :]

    def around(ref, t, first=0, n=rows):
        return ref[t, pl.ds(SUBS + first - 1, n), :] + ref[t, pl.ds(SUBS + first + 1, n), :]

    def spot(t):
        return t // tiles

    def product(values, pieces, w, width):
        n = values[0].shape[0]
        parts = [split(v, pieces) for v in values]
        pair = jnp.concatenate([jnp.concatenate(p[:2], axis=1) for p in parts], axis=0)
        out = jnp.dot(pair, w[:, pl.ds(0, width)], preferred_element_type=f32)
        if pieces == 3:
            last = jnp.concatenate([p[2] for p in parts], axis=0)
            out = out + jnp.dot(last, w[pl.ds(0, LANES), pl.ds(0, width)], preferred_element_type=f32)

        def get(i, k):
            return out[i * n : (i + 1) * n, k * LANES : (k + 1) * LANES]

        return get

    def halves(n):
        return jnp.broadcast_to(low_half[:1], (n, LANES))

    def cross(get, i, k, k_up, count_, n):
        none = jnp.zeros((n, LANES), f32)
        lower = get(i - 1, k_up) if i > 0 else none
        upper = get(i + 1, k) if i < count_ - 1 else none
        return lower, upper

    def blend(get, i, k, amount, n):
        lower, upper = cross(get, i, k, k, amount, n)
        return jnp.where(halves(n), lower, upper)

    low_wall = jnp.where(jnp.logical_and(lane < edge, grp == 0), 1.0, 0.0)
    high_wall = jnp.where(jnp.logical_and(lane >= LANES - edge, grp == n_grp - 1), 1.0, 0.0)

    def walls(value, x, t):
        n = value.shape[0]
        if t == mine[0]:
            value = value - x * jnp.broadcast_to(low_wall[:1], (n, LANES))
        if t == mine[-1]:
            value = value - x * jnp.broadcast_to(high_wall[:1], (n, LANES))
        return value

    def smooth():
        get = product([body(rhs, t) for t in range(wide)], 2, fine_w, 4 * LANES)
        seconds = []
        for t in range(wide):
            r = body(rhs, t)
            first = get(t, 0) + blend(get, t, 1, wide, rows)
            seconds.append(walls(get(t, 2) + blend(get, t, 3, wide, rows), r, t))
            near = around(rhs, t)
            pre[t, pl.ds(SUBS, rows), :] = 9.0 * r + near + 0.5 * first
            gather[t, pl.ds(SUBS, rows), :] = mask[1] * (first + near)
        for t in range(wide):
            other[t, pl.ds(SUBS, rows), :] = seconds[t] + around(gather, t)

    def reflect(q, high):
        turned = pltpu.roll(q, LANES // 2, 1)
        n = q.shape[0]
        at = lax.broadcasted_iota(jnp.int32, (n, LANES), 1) // (2 * edge)
        near, far = (1, 2) if high else (2, 1)
        return jnp.where(at == near, -turned, jnp.where(at == far, -q, 0.0))

    def correct():
        qs = []
        for t in range(wide):
            q = (
                other[t, pl.ds(SUBS, crows, stride=2), :] + other[t, pl.ds(SUBS + 1, crows, stride=2), :]
            )
            qs.append(cmask[spot(t)] * q)
        left, right = mids[0], mids[-1]
        qs[left] = jnp.where(has(has_left), qs[left], reflect(qs[mine[0]], False))
        qs[right] = jnp.where(has(has_right), qs[right], reflect(qs[mine[-1]], True))
        get = product(qs, 2, coarse_w, 8 * LANES)
        b0, b1, b2 = {}, {}, {}
        for t in mids:
            c = get(t, 0)
            j1 = get(t, 1) + blend(get, t, 4, wide, crows)
            j2 = get(t, 2) + blend(get, t, 5, wide, crows)
            j3 = get(t, 3) + (get(t - 1, 7) + get(t + 1, 6))
            coarse[t, pl.ds(SUBS, crows), :] = c
            b0[t] = 729.0 * c + 81.0 * j1 + (9.0 * j2 + j3)
            b1[t] = 81.0 * c + 18.0 * j1 + 3.0 * j2
            b2[t] = 9.0 * c + 3.0 * j1
        for t in mids:
            ea[t, pl.ds(SUBS, crows), :] = cmask[1] * (b2[t] + around(coarse, t, 0, crows))
        for t in mids:
            eb[t, pl.ds(SUBS, crows), :] = cmask[1] * (b1[t] + around(ea, t, 0, crows))
        return {t: b0[t] + around(eb, t, 0, crows) for t in mids}

    scale = CSTEP * STEP * STEP * STEP / 8.0
    square = STEP * STEP

    def tally(e):
        acc = zero
        for t in mine:
            r, q, v = (body(ref, t, edge, planes) for ref in (rhs, other, pre))
            acc = acc + jnp.sum((own[...] * (r + square * q) * v).reshape(-1, SUBS, LANES), axis=0)
            ce = coarse[t, pl.ds(SUBS + half, slots * half), :] * e[t][half : half + slots * half]
            ce = ce.reshape(slots, half // SUBS, SUBS, LANES).sum(axis=1)
            for s in range(slots):
                acc = acc + (0.25 * scale * square) * own[pl.ds(s * edge, SUBS), :] * ce[s]
        return square * acc

    def finish(e, again):
        low, n = SUBS, rows - 2 * SUBS
        for t in mids:
            for up in (0, 1):
                gather[t, pl.ds(SUBS + up, crows, stride=2), :] = e[t]
        for t in mids:
            other[t, pl.ds(SUBS + low, n), :] = mask[spot(t), pl.ds(low, n), :] * (
                body(pre, t, low, n) + scale * body(gather, t, low, n)
            )
        get = product([body(other, t, low, n) for t in mids], 3, fine_w, 4 * LANES)
        out = {}
        for i, t in enumerate(mids):
            first = get(i, 0) + blend(get, i, 1, len(mids), n)
            x = body(other, t, low, n)
            gather[t, pl.ds(SUBS + low, n), :] = mask[1, pl.ds(low, n), :] * (first + around(other, t, low, n))
        for i, t in enumerate(mids):
            if not again and t not in mine:
                continue
            x = body(other, t, low, n)
            second = walls(get(i, 2) + blend(get, i, 3, len(mids), n), x, t)
            out[t] = body(pre, t, low, n) + square * (second + around(gather, t, low, n))
        if again:
            for t in mids:
                gather[t, pl.ds(SUBS + low, n), :] = mask[spot(t), pl.ds(low, n), :] * out[t]
        skip = edge - low
        return [own[...] * out[t][skip : skip + planes] for t in mine]

    def laplace():
        get = product([body(gather, t, edge, planes) for t in mids], 3, fine_w, 2 * LANES)
        out = []
        for i, t in enumerate(mids):
            if t in mine:
                first = get(i, 0) + blend(get, i, 1, len(mids), planes)
                value = 9.0 * body(gather, t, edge, planes) - around(gather, t, edge, planes) - 0.5 * first
                out.append(square * (own[...] * value))
        return out

    count_copy.wait()
    count = counts[0]
    pack(0, source_ref)
    if gossip:
        near = (1 + one(sfc > 0) + one(sfc < n_sfc - 1)) * (1 + one(grp > 0) + one(grp < n_grp - 1))
        pl.semaphore_wait(barrier, near - 1)
    else:
        pl.semaphore_wait(barrier, everyone - 1)
    start(0, source_ref)

    for g, present in enumerate((has_left, 1, has_right)):
        for s in range(slots + 2):
            if s == 0:
                ok = has_below
            else:
                ok = one(count >= s) + one(count == s - 1) * has_above
            value = jnp.full((SUBS, LANES), ok * present, jnp.int32).astype(f32)
            for h in range(edge // SUBS):
                mask[g, pl.ds(s * edge + h * SUBS, SUBS), :] = value
            for h in range(half // SUBS):
                cmask[g, pl.ds(s * half + h * SUBS, SUBS), :] = value
    for s in range(slots):
        value = jnp.full((SUBS, LANES), one(count > s), jnp.int32).astype(f32)
        for h in range(edge // SUBS):
            own[pl.ds(s * edge + h * SUBS, SUBS), :] = value
    for copy in weight_copies:
        copy.wait()

    receive(0, source_ref)
    greet_far(0, 2)
    unpack(0, source_ref)
    smooth()
    firsts = finish(correct(), True)
    images = laplace()
    for i, value in enumerate(images):
        image_buf[:, pl.ds(i * LANES, LANES)] = value
    pack(1, image_buf)
    hear_far(0, 2)
    sent(0, source_ref)
    start(1, image_buf)
    acc_rz, acc_curv = zero, zero
    for i in range(tiles):
        cols = pl.ds(i * LANES, LANES)
        value = square * firsts[i]
        image = images[i]
        source = body(rhs, mine[i], edge, planes) * own[...]
        first_ref[:, cols] = value
        image_ref[:, cols] = image
        source_out[:, cols] = source
        acc_rz = acc_rz + jnp.sum((source * value).reshape(-1, SUBS, LANES), axis=0)
        acc_curv = acc_curv + jnp.sum((value * image).reshape(-1, SUBS, LANES), axis=0)
    row = lax.broadcasted_iota(jnp.int32, (1, LANES), 1)

    def whole(acc):
        return jnp.sum(jnp.sum(acc, axis=0, keepdims=True), axis=1, keepdims=True)

    rz, curv = whole(acc_rz), whole(acc_curv)
    known = jnp.where(row == 0, rz, jnp.where(row == 1, curv, 0.0))
    receive(1, image_buf)
    greet_far(1, 4)
    unpack(1, image_buf)

    def send(slot, device):
        return pltpu.make_async_remote_copy(
            src_ref=part, dst_ref=red.at[slot], send_sem=red_sem.at[0],
            recv_sem=red_sem.at[1], device_id=device, device_id_type=MESH,
        )

    smooth()
    e = correct()
    value = jnp.where(row == 2, whole(tally(e)), known)
    part[...] = value
    red[me] = value
    hear_far(1, 4)

    def go(i, carry):
        peer, device = place(i)
        send(me, device).start()
        return carry

    lax.fori_loop(1, everyone, go, 0)
    for i, value in enumerate(finish(e, False)):
        w_ref[:, pl.ds(i * LANES, LANES)] = square * value
    sent(1, image_buf)

    rest = red.at[pl.ds(0, everyone - 1)]
    pltpu.make_async_copy(rest, rest, red_sem.at[0]).wait()
    pltpu.make_async_copy(rest, rest, red_sem.at[1]).wait()
    sums = jnp.sum(red[...], axis=0)

    def pick(i):
        return jnp.sum(jnp.where(row == i, sums, 0.0), axis=1, keepdims=True)

    alpha = pick(0) / pick(1)
    ratio = pick(2) / pick(1)
    scale_ref[...] = jnp.concatenate(
        [jnp.broadcast_to(alpha, (1, LANES)), jnp.broadcast_to(ratio, (1, LANES))], axis=0
    )


def combine(first, image, w, source, scale, solution_ref, residual_ref, direction_ref):
    alpha = scale[0:1, 0:1]
    ratio = scale[1:2, 0:1]
    solution_ref[...] = alpha * first[...]
    residual_ref[...] = source[...] - alpha * image[...]
    direction_ref[...] = alpha * (ratio * first[...] - w[...])


def shards(n_sfc, n_grp, source, layer_counts):
    slots, edge, width = source.shape
    planes, tiles = slots * edge, width // LANES
    rows, crows = (slots + 2) * edge, (slots + 2) * edge // 2
    f32 = jnp.float32
    vmem = pltpu.VMEM
    dma = pltpu.SemaphoreType.DMA
    n = n_sfc * n_grp
    out = jax.ShapeDtypeStruct((planes, width), f32)
    fine = vmem((3 * tiles, rows + 2 * SUBS, LANES), f32)
    coarse = vmem((3 * tiles, crows + 2 * SUBS, LANES), f32)
    parts = pl.pallas_call(
        functools.partial(kernel, (slots, edge, tiles, n_sfc, n_grp)),
        out_shape=(out, out, out, out, jax.ShapeDtypeStruct((2, LANES), f32)),
        in_specs=[pl.BlockSpec(memory_space=pltpu.HBM)] * 3,
        out_specs=[pl.BlockSpec(memory_space=pltpu.VMEM)] * 5,
        scratch_shapes=[
            vmem((planes, width), f32),
            vmem((planes, width), f32),
            pltpu.SMEM((1,), jnp.int32),
            vmem((2 * LANES, 4 * LANES), jnp.bfloat16),
            vmem((2 * LANES, 8 * LANES), jnp.bfloat16),
            fine, fine, fine, fine, coarse, coarse, coarse,
            vmem((3, rows, LANES), f32),
            vmem((3, crows, LANES), f32),
            vmem((planes, LANES), f32),
            vmem((2, 2, 5, SUBS, LANES), f32),
            vmem((2, 2, planes, width), f32),
            vmem((2, 3, 3, SUBS, LANES), f32),
            vmem((2, 3, 3, SUBS, LANES), f32),
            vmem((1, LANES), f32),
            vmem((n, 1, LANES), f32),
            dma((6,)),
            dma((len(WAYS),)),
            dma((2, len(WAYS))),
            dma((2,)),
            pltpu.SemaphoreType.REGULAR((2,)),
        ],
        compiler_params=pltpu.CompilerParams(
            collective_id=0, has_side_effects=True, vmem_limit_bytes=16 * 1024 * 1024
        ),
        name="pcg",
    )(layer_counts, source.reshape(planes, width), jnp.asarray(weights(edge)))
    outs = pl.pallas_call(
        combine,
        out_shape=(out, out, out),
        in_specs=[pl.BlockSpec(memory_space=pltpu.VMEM)] * 5,
        out_specs=[pl.BlockSpec(memory_space=pltpu.VMEM)] * 3,
        compiler_params=pltpu.CompilerParams(vmem_limit_bytes=16 * 1024 * 1024),
        name="combine",
    )(*parts)
    return tuple(o.reshape(source.shape) for o in outs)


def solution(mesh):
    n_sfc, n_grp = mesh.shape["sfc"], mesh.shape["grp"]
    return jax.shard_map(
        functools.partial(shards, n_sfc, n_grp),
        mesh=mesh,
        in_specs=(P("sfc", None, "grp"), P("sfc")),
        out_specs=(P("sfc", None, "grp"), P("sfc", None, "grp"), P("sfc", None, "grp")),
        check_vma=False,
    )
```

time: 28.1 us -> 23.5 us (0.84)
  Pallas kernels: 25.8 us -> 20.2 us
  local copies, waits for them, and re-layouts: 0.83 us -> 1.83 us
    pallas_call x1, Pallas kernels: 25.1 us -> 19.4 us  [shards(): pl.pallas_call(functools.partial(kernel, (slots, edge, tiles, n_sfc, n_gr...]
    unnamed x2 -> x4, local copies, waits for them, and re-layouts: 0.83 us -> 1.83 us
where the time goes in v1:
time: 23.5 us; the launch traced here: 23.3 us
  Pallas kernels  20.2 us (86%)
  local copies, waits for them, and re-layouts  1.83 us (8%)
  between operations  1.29 us (5%)
    pallas_call x1, Pallas kernels, shards(): pl.pallas_call(functools.partial(kernel, (slots, edge, tiles, n_sfc, n_gr...  19.4 us
    unnamed x4, local copies, waits for them, and re-layouts  1.83 us
    pallas_call x1, Pallas kernels, shards(): pl.pallas_call(combine, out_shape=(out, out, out), in_specs=[pl.BlockSpec...  0.72 us

profile of v1, /device:TPU:0, one launch (start us, length us, event | category | flops | bytes accessed | tf_op | source)
XLA Modules:
  0.0 23.3 jit_solution(6914143519563122673)
XLA Ops:
  1.3 0.0 copy-start
  1.3 1.0 %copy-done = bf16[128,1536]{1,0:T(8,128)(2,1)S(1)} copy-done((bf16[128,1536]{1,0:T(8,128)(2,1)S(1)}, bf16[128,1536]{1,0:T(8,128)(2,1)}, u32[]{:S(2)}) %copy-start) | copy-done | bytes 393240
  2.3 0.0 copy-start.1
  2.3 0.8 %copy-done.1 = f32[4,16,256]{2,1,0:T(8,128)S(1)} copy-done((f32[4,16,256]{2,1,0:T(8,128)S(1)}, f32[4,16,256]{2,1,0:T(8,128)}, u32[]{:S(2)}) %copy-start.1) | copy-done | bytes 65560
  3.1 19.4 %pcg.1 = (f32[64,256]{1,0:T(8,128)S(1)}, f32[64,256]{1,0:T(8,128)S(1)}, f32[64,256]{1,0:T(8,128)S(1)}, f32[64,256]{1,0:T(8,128)S(1)}, f32[2,128]{1,0:T(2,128)S(1)}) custom-call(s32[1]{0:T(128)S(6)} %copy.6.count_hbm, f32[64,256]{1,0:T(8,128)S(1)} %bitcast.4, bf16[128,1536]{1,0:T(8,128)(2,1)S(1)} %copy-done), custom_call_target="tpu_custom_call" | custom-call | tf_op jit(solution)/shard_map/pcg/pallas_call | solution.py:527
  22.6 0.7 %combine.1 = (f32[64,256]{1,0:T(8,128)}, f32[64,256]{1,0:T(8,128)}, f32[64,256]{1,0:T(8,128)}) custom-call(f32[64,256]{1,0:T(8,128)S(1)} %get-tuple-element.11.first, f32[64,256]{1,0:T(8,128)S(1)} %get-tuple-element.12.image, f32[64,256]{1,0:T(8,128)S(1)} %get-tuple-element.13.w, f32[64,256]{1,0:T(8,128)S(1)} %get-tuple-element.14.source, ...), custom_call_target="tpu_custom_call" | custom-call | tf_op jit(solution)/shard_map/combine/pallas_call | solution.py:559
Async XLA Ops:
  1.3 1.0 %copy-start = (bf16[128,1536]{1,0:T(8,128)(2,1)S(1)}, bf16[128,1536]{1,0:T(8,128)(2,1)}, u32[]{:S(2)}) copy-start(bf16[128,1536]{1,0:T(8,128)(2,1)} %constant.2.clone.weight_hbm) | copy-start | bytes 1179652
  2.3 0.8 %copy-start.1 = (f32[4,16,256]{2,1,0:T(8,128)S(1)}, f32[4,16,256]{2,1,0:T(8,128)}, u32[]{:S(2)}) copy-start(f32[4,16,256]{2,1,0:T(8,128)} %param.3) | copy-start | bytes 196612

commit v2 on v1

--- a/solution.py
+++ b/solution.py
@@ -92,9 +92,7 @@
         return carry
 
     source_copy = pltpu.make_async_copy(source_hbm, source_ref, local_sem.at[1])
-    count_copy = pltpu.make_async_copy(count_hbm, counts, local_sem.at[0])
     source_copy.start()
-    count_copy.start()
     weight_copies = []
     for i, (ref, at, width) in enumerate(((fine_w, 0, 4 * LANES), (coarse_w, 4 * LANES, 8 * LANES))):
         for up in (0, 1):
@@ -118,18 +116,25 @@
     def one(flag):
         return jnp.where(flag, 1, 0)
 
-    def greet_far(rnd, far):
-        if gossip and far < n_sfc:
-            for ds in (far, -far):
-                @pl.when(sfc + ds < n_sfc if ds > 0 else sfc + ds >= 0)
-                def _(ds=ds):
+    rounds = (((2, 0), (-2, 0)), ((4, 0), (-4, 0)), ((0, 1), (0, -1)))
+
+    def inside(ds, dg):
+        flag = sfc + ds < n_sfc if ds >= 0 else sfc + ds >= 0
+        return jnp.logical_and(flag, grp + dg < n_grp if dg >= 0 else grp + dg >= 0)
+
+    def tell(rnd):
+        if gossip:
+            for ds, dg in rounds[rnd]:
+                @pl.when(inside(ds, dg))
+                def _(ds=ds, dg=dg):
                     pl.semaphore_signal(
-                        hello.at[rnd], inc=1, device_id={"sfc": sfc + ds}, device_id_type=MESH
+                        hello.at[rnd], inc=1, device_id={"sfc": sfc + ds, "grp": grp + dg},
+                        device_id_type=MESH,
                     )
 
-    def hear_far(rnd, far):
-        if gossip and far < n_sfc:
-            pl.semaphore_wait(hello.at[rnd], one(sfc + far < n_sfc) + one(sfc >= far))
+    def hear(rnd):
+        if gossip:
+            pl.semaphore_wait(hello.at[rnd], sum(one(inside(ds, dg)) for ds, dg in rounds[rnd]))
 
     lane = lax.broadcasted_iota(jnp.int32, (SUBS, LANES), 1)
     low_half = lane < LANES // 2
@@ -405,8 +410,7 @@
                 out.append(square * (own[...] * value))
         return out
 
-    count_copy.wait()
-    count = counts[0]
+    count = count_hbm[0]
     pack(0, source_ref)
     if gossip:
         near = (1 + one(sfc > 0) + one(sfc < n_sfc - 1)) * (1 + one(grp > 0) + one(grp < n_grp - 1))
@@ -434,7 +438,7 @@
         copy.wait()
 
     receive(0, source_ref)
-    greet_far(0, 2)
+    tell(0)
     unpack(0, source_ref)
     smooth()
     firsts = finish(correct(), True)
@@ -442,9 +446,10 @@
     for i, value in enumerate(images):
         image_buf[:, pl.ds(i * LANES, LANES)] = value
     pack(1, image_buf)
-    hear_far(0, 2)
     sent(0, source_ref)
     start(1, image_buf)
+    hear(0)
+    tell(1)
     acc_rz, acc_curv = zero, zero
     for i in range(tiles):
         cols = pl.ds(i * LANES, LANES)
@@ -463,8 +468,9 @@
 
     rz, curv = whole(acc_rz), whole(acc_curv)
     known = jnp.where(row == 0, rz, jnp.where(row == 1, curv, 0.0))
+    hear(1)
+    tell(2)
     receive(1, image_buf)
-    greet_far(1, 4)
     unpack(1, image_buf)
 
     def send(slot, device):
@@ -478,14 +484,23 @@
     value = jnp.where(row == 2, whole(tally(e)), known)
     part[...] = value
     red[me] = value
-    hear_far(1, 4)
-
-    def go(i, carry):
-        peer, device = place(i)
-        send(me, device).start()
-        return carry
-
-    lax.fori_loop(1, everyone, go, 0)
+    hear(2)
+
+    if everyone <= 64:
+        turn = jnp.where(2 * sfc >= n_sfc, 1, n_sfc - 1)
+        grps = [lax.rem(grp + i, n_grp) for i in range(n_grp)]
+        for ds in (*range(1, n_sfc), 0):
+            there_sfc = lax.rem(sfc + ds * turn, n_sfc)
+            for dg in range(n_grp):
+                if ds or dg:
+                    send(me, {"sfc": there_sfc, "grp": grps[dg]}).start()
+    else:
+        def go(i, carry):
+            peer, device = place(i)
+            send(me, device).start()
+            return carry
+
+        lax.fori_loop(1, everyone, go, 0)
     for i, value in enumerate(finish(e, False)):
         w_ref[:, pl.ds(i * LANES, LANES)] = square * value
     sent(1, image_buf)
@@ -527,7 +542,7 @@
     parts = pl.pallas_call(
         functools.partial(kernel, (slots, edge, tiles, n_sfc, n_grp)),
         out_shape=(out, out, out, out, jax.ShapeDtypeStruct((2, LANES), f32)),
-        in_specs=[pl.BlockSpec(memory_space=pltpu.HBM)] * 3,
+        in_specs=[pl.BlockSpec(memory_space=pltpu.SMEM)] + [pl.BlockSpec(memory_space=pltpu.HBM)] * 2,
         out_specs=[pl.BlockSpec(memory_space=pltpu.VMEM)] * 5,
         scratch_shapes=[
             vmem((planes, width), f32),
@@ -549,13 +564,13 @@
             dma((len(WAYS),)),
             dma((2, len(WAYS))),
             dma((2,)),
-            pltpu.SemaphoreType.REGULAR((2,)),
+            pltpu.SemaphoreType.REGULAR((3,)),
         ],
         compiler_params=pltpu.CompilerParams(
             collective_id=0, has_side_effects=True, vmem_limit_bytes=16 * 1024 * 1024
         ),
         name="pcg",
-    )(layer_counts, source.reshape(planes, width), jnp.asarray(weights(edge)))
+    )(layer_counts, pltpu.with_memory_space_constraint(source.reshape(planes, width), pltpu.HBM), pltpu.with_memory_space_constraint(jnp.asarray(weights(edge)), pltpu.HBM))
     outs = pl.pallas_call(
         combine,
         out_shape=(out, out, out),

time: 23.5 us -> 20.8 us (0.89)
  local copies, waits for them, and re-layouts: 1.83 us -> 0 us
  Pallas kernels: 20.2 us -> 19.3 us
    unnamed x4 -> x0, local copies, waits for them, and re-layouts: 1.83 us -> none
    pallas_call x1, Pallas kernels: 19.4 us -> 18.6 us  [shards(): pl.pallas_call(functools.partial(kernel, (slots, edge, tiles, n_sfc, n_gr...]
where the time goes in v2:
time: 20.8 us; the launch traced here: 20.6 us
  Pallas kernels  19.3 us (93%)
  between operations  1.28 us (6%)
    pallas_call x1, Pallas kernels, shards(): pl.pallas_call(functools.partial(kernel, (slots, edge, tiles, n_sfc, n_gr...  18.6 us
    pallas_call x1, Pallas kernels, shards(): pl.pallas_call(combine, out_shape=(out, out, out), in_specs=[pl.BlockSpec...  0.72 us

profile of v2, /device:TPU:0, one launch (start us, length us, event | category | flops | bytes accessed | tf_op | source)
XLA Modules:
  0.0 20.6 jit_solution(13818210041067667387)
XLA Ops:
  1.3 18.6 %pcg.1 = (f32[64,256]{1,0:T(8,128)S(1)}, f32[64,256]{1,0:T(8,128)S(1)}, f32[64,256]{1,0:T(8,128)S(1)}, f32[64,256]{1,0:T(8,128)S(1)}, f32[2,128]{1,0:T(2,128)S(1)}) custom-call(s32[1]{0:T(128)S(6)} %copy.6.count_hbm, f32[64,256]{1,0:T(8,128)} %bitcast.4, bf16[128,1536]{1,0:T(8,128)(2,1)} %constant.2.clone.weight_hbm), custom_call_target="tpu_custom_call" | custom-call | tf_op jit(solution)/shard_map/pcg/pallas_call | solution.py:542
  19.9 0.7 %combine.1 = (f32[64,256]{1,0:T(8,128)}, f32[64,256]{1,0:T(8,128)}, f32[64,256]{1,0:T(8,128)}) custom-call(f32[64,256]{1,0:T(8,128)S(1)} %get-tuple-element.11.first, f32[64,256]{1,0:T(8,128)S(1)} %get-tuple-element.12.image, f32[64,256]{1,0:T(8,128)S(1)} %get-tuple-element.13.w, f32[64,256]{1,0:T(8,128)S(1)} %get-tuple-element.14.source, ...), custom_call_target="tpu_custom_call" | custom-call | tf_op jit(solution)/shard_map/combine/pallas_call | solution.py:574

commit v3 on v2

--- a/solution.py
+++ b/solution.py
@@ -54,9 +54,9 @@
 
 def kernel(
     dims, count_hbm, source_hbm, weight_hbm, first_ref, image_ref, w_ref, source_out, scale_ref,
-    source_ref, image_buf, counts, fine_w, coarse_w, rhs, pre, gather, other, coarse, ea, eb,
-    mask, cmask, own, packed, side, below, above, part, red, local_sem,
-    send_sem, recv_sem, red_sem, hello,
+    source_ref, image_buf, weight_ref, rhs, pre, gather, other, coarse, ea, eb,
+    mask, cmask, own, packed, side, below, above, part, red, dummy, local_sem,
+    trade_sem, red_sem, hello,
 ):
     slots, edge, tiles, n_sfc, n_grp = dims
     half = edge // 2
@@ -91,17 +91,12 @@
         pl.semaphore_signal(barrier, inc=1, device_id=place(i)[1], device_id_type=MESH)
         return carry
 
-    source_copy = pltpu.make_async_copy(source_hbm, source_ref, local_sem.at[1])
+    source_copy = pltpu.make_async_copy(source_hbm, source_ref, local_sem.at[0])
     source_copy.start()
-    weight_copies = []
-    for i, (ref, at, width) in enumerate(((fine_w, 0, 4 * LANES), (coarse_w, 4 * LANES, 8 * LANES))):
-        for up in (0, 1):
-            copy = pltpu.make_async_copy(
-                weight_hbm.at[:, pl.ds(at, width)], ref.at[pl.ds(up * LANES, LANES), :],
-                local_sem.at[2 + 2 * i + up],
-            )
-            copy.start()
-            weight_copies.append(copy)
+    for up in (0, 1):
+        pltpu.make_async_copy(
+            weight_hbm, weight_ref.at[pl.ds(up * LANES, LANES), :], local_sem.at[1]
+        ).start()
     if gossip:
         for ds, dg in WAYS:
             @pl.when(there(ds, dg))
@@ -162,7 +157,7 @@
 
     source_copy.wait()
 
-    def copies(e, i, ds, dg, src):
+    def copies(e, ds, dg, src):
         gpos = 1 - dg
         if ds == 0:
             source, target = src, side.at[e, gpos // 2]
@@ -171,28 +166,32 @@
             source = packed.at[e, int(ds > 0), pl.ds(tile, amount)]
             target = (below if ds > 0 else above).at[e, gpos, pl.ds(0, amount)]
         return pltpu.make_async_remote_copy(
-            src_ref=source, dst_ref=target, send_sem=send_sem.at[i],
-            recv_sem=recv_sem.at[e, i], device_id={"sfc": sfc + ds, "grp": grp + dg},
+            src_ref=source, dst_ref=target, send_sem=trade_sem.at[0],
+            recv_sem=trade_sem.at[1 + e], device_id={"sfc": sfc + ds, "grp": grp + dg},
             device_id_type=MESH,
         )
 
     def start(e, src):
-        for i, (ds, dg) in enumerate(WAYS):
+        for ds, dg in WAYS:
             @pl.when(there(ds, dg))
-            def _(i=i, ds=ds, dg=dg):
-                copies(e, i, ds, dg, src).start()
-
-    def receive(e, src):
-        for i, (ds, dg) in enumerate(WAYS):
-            @pl.when(there(-ds, -dg))
-            def _(i=i, ds=ds, dg=dg):
-                copies(e, i, ds, dg, src).wait_recv()
-
-    def sent(e, src):
-        for i, (ds, dg) in enumerate(WAYS):
-            @pl.when(there(ds, dg))
-            def _(i=i, ds=ds, dg=dg):
-                copies(e, i, ds, dg, src).wait_send()
+            def _(ds=ds, dg=dg):
+                copies(e, ds, dg, src).start()
+
+    def settle(sem):
+        column = slots * edge * tiles // SUBS
+        for beside in range(3):
+            for along in range(3):
+                total = beside * column + along * (3 + 2 * beside)
+
+                @pl.when(
+                    jnp.logical_and(
+                        has_left + has_right == beside, has_below + has_above == along
+                    )
+                )
+                def _(total=total):
+                    if total:
+                        ref = dummy.at[pl.ds(0, total)]
+                        pltpu.make_async_copy(ref, ref, trade_sem.at[sem]).wait()
 
     def pack(e, src):
         cut = SUBS // 2
@@ -274,14 +273,14 @@
     def spot(t):
         return t // tiles
 
-    def product(values, pieces, w, width):
+    def product(values, pieces, at, width):
         n = values[0].shape[0]
         parts = [split(v, pieces) for v in values]
         pair = jnp.concatenate([jnp.concatenate(p[:2], axis=1) for p in parts], axis=0)
-        out = jnp.dot(pair, w[:, pl.ds(0, width)], preferred_element_type=f32)
+        out = jnp.dot(pair, weight_ref[:, pl.ds(at, width)], preferred_element_type=f32)
         if pieces == 3:
             last = jnp.concatenate([p[2] for p in parts], axis=0)
-            out = out + jnp.dot(last, w[pl.ds(0, LANES), pl.ds(0, width)], preferred_element_type=f32)
+            out = out + jnp.dot(last, weight_ref[pl.ds(0, LANES), pl.ds(at, width)], preferred_element_type=f32)
 
         def get(i, k):
             return out[i * n : (i + 1) * n, k * LANES : (k + 1) * LANES]
@@ -313,7 +312,7 @@
         return value
 
     def smooth():
-        get = product([body(rhs, t) for t in range(wide)], 2, fine_w, 4 * LANES)
+        get = product([body(rhs, t) for t in range(wide)], 2, 0, 4 * LANES)
         seconds = []
         for t in range(wide):
             r = body(rhs, t)
@@ -342,7 +341,7 @@
         left, right = mids[0], mids[-1]
         qs[left] = jnp.where(has(has_left), qs[left], reflect(qs[mine[0]], False))
         qs[right] = jnp.where(has(has_right), qs[right], reflect(qs[mine[-1]], True))
-        get = product(qs, 2, coarse_w, 8 * LANES)
+        get = product(qs, 2, 4 * LANES, 8 * LANES)
         b0, b1, b2 = {}, {}, {}
         for t in mids:
             c = get(t, 0)
@@ -382,7 +381,7 @@
             other[t, pl.ds(SUBS + low, n), :] = mask[spot(t), pl.ds(low, n), :] * (
                 body(pre, t, low, n) + scale * body(gather, t, low, n)
             )
-        get = product([body(other, t, low, n) for t in mids], 3, fine_w, 4 * LANES)
+        get = product([body(other, t, low, n) for t in mids], 3, 0, 4 * LANES)
         out = {}
         for i, t in enumerate(mids):
             first = get(i, 0) + blend(get, i, 1, len(mids), n)
@@ -401,7 +400,7 @@
         return [own[...] * out[t][skip : skip + planes] for t in mine]
 
     def laplace():
-        get = product([body(gather, t, edge, planes) for t in mids], 3, fine_w, 2 * LANES)
+        get = product([body(gather, t, edge, planes) for t in mids], 3, 0, 2 * LANES)
         out = []
         for i, t in enumerate(mids):
             if t in mine:
@@ -434,10 +433,9 @@
         value = jnp.full((SUBS, LANES), one(count > s), jnp.int32).astype(f32)
         for h in range(edge // SUBS):
             own[pl.ds(s * edge + h * SUBS, SUBS), :] = value
-    for copy in weight_copies:
-        copy.wait()
-
-    receive(0, source_ref)
+    pltpu.make_async_copy(weight_ref, weight_ref, local_sem.at[1]).wait()
+
+    settle(1)
     tell(0)
     unpack(0, source_ref)
     smooth()
@@ -446,7 +444,7 @@
     for i, value in enumerate(images):
         image_buf[:, pl.ds(i * LANES, LANES)] = value
     pack(1, image_buf)
-    sent(0, source_ref)
+    settle(0)
     start(1, image_buf)
     hear(0)
     tell(1)
@@ -470,7 +468,7 @@
     known = jnp.where(row == 0, rz, jnp.where(row == 1, curv, 0.0))
     hear(1)
     tell(2)
-    receive(1, image_buf)
+    settle(2)
     unpack(1, image_buf)
 
     def send(slot, device):
@@ -503,7 +501,7 @@
         lax.fori_loop(1, everyone, go, 0)
     for i, value in enumerate(finish(e, False)):
         w_ref[:, pl.ds(i * LANES, LANES)] = square * value
-    sent(1, image_buf)
+    settle(0)
 
     rest = red.at[pl.ds(0, everyone - 1)]
     pltpu.make_async_copy(rest, rest, red_sem.at[0]).wait()
@@ -547,9 +545,7 @@
         scratch_shapes=[
             vmem((planes, width), f32),
             vmem((planes, width), f32),
-            pltpu.SMEM((1,), jnp.int32),
-            vmem((2 * LANES, 4 * LANES), jnp.bfloat16),
-            vmem((2 * LANES, 8 * LANES), jnp.bfloat16),
+            vmem((2 * LANES, 12 * LANES), jnp.bfloat16),
             fine, fine, fine, fine, coarse, coarse, coarse,
             vmem((3, rows, LANES), f32),
             vmem((3, crows, LANES), f32),
@@ -560,9 +556,9 @@
             vmem((2, 3, 3, SUBS, LANES), f32),
             vmem((1, LANES), f32),
             vmem((n, 1, LANES), f32),
-            dma((6,)),
-            dma((len(WAYS),)),
-            dma((2, len(WAYS))),
+            vmem((2 * planes * tiles // SUBS + 14, SUBS, LANES), f32),
+            dma((2,)),
+            dma((3,)),
             dma((2,)),
             pltpu.SemaphoreType.REGULAR((3,)),
         ],

time: 20.8 us -> 20.5 us (0.986)
    pallas_call x1, Pallas kernels: 18.6 us -> 18.4 us  [shards(): pl.pallas_call(functools.partial(kernel, (slots, edge, tiles, n_sfc, n_gr...]
where the time goes in v3:
time: 20.5 us; the launch traced here: 20.4 us
  Pallas kernels  19.1 us (93%)
  between operations  1.28 us (6%)
    pallas_call x1, Pallas kernels, shards(): pl.pallas_call(functools.partial(kernel, (slots, edge, tiles, n_sfc, n_gr...  18.4 us
    pallas_call x1, Pallas kernels, shards(): pl.pallas_call(combine, out_shape=(out, out, out), in_specs=[pl.BlockSpec...  0.72 us

profile of v3, /device:TPU:0, one launch (start us, length us, event | category | flops | bytes accessed | tf_op | source)
XLA Modules:
  0.0 20.4 jit_solution(121600752877981488)
XLA Ops:
  1.3 18.4 %pcg.1 = (f32[64,256]{1,0:T(8,128)S(1)}, f32[64,256]{1,0:T(8,128)S(1)}, f32[64,256]{1,0:T(8,128)S(1)}, f32[64,256]{1,0:T(8,128)S(1)}, f32[2,128]{1,0:T(2,128)S(1)}) custom-call(s32[1]{0:T(128)S(6)} %copy.6.count_hbm, f32[64,256]{1,0:T(8,128)} %bitcast.4, bf16[128,1536]{1,0:T(8,128)(2,1)} %constant.2.clone.weight_hbm), custom_call_target="tpu_custom_call" | custom-call | tf_op jit(solution)/shard_map/pcg/pallas_call | solution.py:540
  19.6 0.7 %combine.1 = (f32[64,256]{1,0:T(8,128)}, f32[64,256]{1,0:T(8,128)}, f32[64,256]{1,0:T(8,128)}) custom-call(f32[64,256]{1,0:T(8,128)S(1)} %get-tuple-element.11.first, f32[64,256]{1,0:T(8,128)S(1)} %get-tuple-element.12.image, f32[64,256]{1,0:T(8,128)S(1)} %get-tuple-element.13.w, f32[64,256]{1,0:T(8,128)S(1)} %get-tuple-element.14.source, ...), custom_call_target="tpu_custom_call" | custom-call | tf_op jit(solution)/shard_map/combine/pallas_call | solution.py:570

commit v4 on v3

--- a/solution.py
+++ b/solution.py
@@ -54,7 +54,7 @@
 
 def kernel(
     dims, count_hbm, source_hbm, weight_hbm, first_ref, image_ref, w_ref, source_out, scale_ref,
-    source_ref, image_buf, weight_ref, rhs, pre, gather, other, coarse, ea, eb,
+    source_ref, image_buf, weight_ref, rhs, pre, gather, other, dual, coarse, ea, eb,
     mask, cmask, own, packed, side, below, above, part, red, dummy, local_sem,
     trade_sem, red_sem, hello,
 ):
@@ -111,7 +111,7 @@
     def one(flag):
         return jnp.where(flag, 1, 0)
 
-    rounds = (((2, 0), (-2, 0)), ((4, 0), (-4, 0)), ((0, 1), (0, -1)))
+    rounds = (((2, 1), (2, -1), (-2, 1), (-2, -1), (0, 1), (0, -1)), ((4, 0), (-4, 0)))
 
     def inside(ds, dg):
         flag = sfc + ds < n_sfc if ds >= 0 else sfc + ds >= 0
@@ -292,8 +292,8 @@
 
     def cross(get, i, k, k_up, count_, n):
         none = jnp.zeros((n, LANES), f32)
-        lower = get(i - 1, k_up) if i > 0 else none
-        upper = get(i + 1, k) if i < count_ - 1 else none
+        lower = get(i - 1, k_up) if 0 < i <= count_ else none
+        upper = get(i + 1, k) if -1 <= i < count_ - 1 else none
         return lower, upper
 
     def blend(get, i, k, amount, n):
@@ -361,19 +361,7 @@
     scale = CSTEP * STEP * STEP * STEP / 8.0
     square = STEP * STEP
 
-    def tally(e):
-        acc = zero
-        for t in mine:
-            r, q, v = (body(ref, t, edge, planes) for ref in (rhs, other, pre))
-            acc = acc + jnp.sum((own[...] * (r + square * q) * v).reshape(-1, SUBS, LANES), axis=0)
-            ce = coarse[t, pl.ds(SUBS + half, slots * half), :] * e[t][half : half + slots * half]
-            ce = ce.reshape(slots, half // SUBS, SUBS, LANES).sum(axis=1)
-            for s in range(slots):
-                acc = acc + (0.25 * scale * square) * own[pl.ds(s * edge, SUBS), :] * ce[s]
-        return square * acc
-
-    def finish(e, again):
-        low, n = SUBS, rows - 2 * SUBS
+    def finish(e, outs, low, n):
         for t in mids:
             for up in (0, 1):
                 gather[t, pl.ds(SUBS + up, crows, stride=2), :] = e[t]
@@ -382,22 +370,25 @@
                 body(pre, t, low, n) + scale * body(gather, t, low, n)
             )
         get = product([body(other, t, low, n) for t in mids], 3, 0, 4 * LANES)
-        out = {}
-        for i, t in enumerate(mids):
-            first = get(i, 0) + blend(get, i, 1, len(mids), n)
-            x = body(other, t, low, n)
-            gather[t, pl.ds(SUBS + low, n), :] = mask[1, pl.ds(low, n), :] * (first + around(other, t, low, n))
-        for i, t in enumerate(mids):
-            if not again and t not in mine:
-                continue
-            x = body(other, t, low, n)
-            second = walls(get(i, 2) + blend(get, i, 3, len(mids), n), x, t)
+        first, out = mids[0], {}
+        near = len(mids)
+        for t in outs:
+            i = t - first
+            if t in mids:
+                value = get(i, 0) + blend(get, i, 1, near, n) + around(other, t, low, n)
+            else:
+                value = blend(get, i, 1, near, n)
+            gather[t, pl.ds(SUBS + low, n), :] = mask[1, pl.ds(low, n), :] * value
+        for t in outs:
+            i = t - first
+            second = blend(get, i, 3, near, n)
+            if t in mids:
+                second = walls(get(i, 2) + second, body(other, t, low, n), t)
             out[t] = body(pre, t, low, n) + square * (second + around(gather, t, low, n))
-        if again:
-            for t in mids:
-                gather[t, pl.ds(SUBS + low, n), :] = mask[spot(t), pl.ds(low, n), :] * out[t]
-        skip = edge - low
-        return [own[...] * out[t][skip : skip + planes] for t in mine]
+        return out
+
+    def owned(out, low):
+        return [own[...] * out[t][edge - low : edge - low + planes] for t in mine]
 
     def laplace():
         get = product([body(gather, t, edge, planes) for t in mids], 3, 0, 2 * LANES)
@@ -439,7 +430,11 @@
     tell(0)
     unpack(0, source_ref)
     smooth()
-    firsts = finish(correct(), True)
+    low, n = SUBS, rows - 2 * SUBS
+    out = finish(correct(), mids, low, n)
+    for t in mids:
+        gather[t, pl.ds(SUBS + low, n), :] = mask[spot(t), pl.ds(low, n), :] * out[t]
+    firsts = owned(out, low)
     images = laplace()
     for i, value in enumerate(images):
         image_buf[:, pl.ds(i * LANES, LANES)] = value
@@ -466,10 +461,23 @@
 
     rz, curv = whole(acc_rz), whole(acc_curv)
     known = jnp.where(row == 0, rz, jnp.where(row == 1, curv, 0.0))
-    hear(1)
-    tell(2)
+
+    for t in range(wide):
+        if t in mine:
+            rhs[t, pl.ds(SUBS, edge), :] = jnp.zeros((edge, LANES), f32)
+            rhs[t, pl.ds(SUBS + edge, planes), :] = images[t - tiles]
+            rhs[t, pl.ds(SUBS + edge + planes, edge), :] = jnp.zeros((edge, LANES), f32)
+        else:
+            rhs[t, pl.ds(SUBS, rows), :] = jnp.zeros((rows, LANES), f32)
+    smooth()
+    out = finish(correct(), range(wide), 0, rows)
+    for t in range(wide):
+        dual[t] = mask[spot(t)] * out[t]
     settle(2)
     unpack(1, image_buf)
+    acc = zero
+    for t in range(wide):
+        acc = acc + jnp.sum((dual[t] * body(rhs, t)).reshape(-1, SUBS, LANES), axis=0)
 
     def send(slot, device):
         return pltpu.make_async_remote_copy(
@@ -477,12 +485,10 @@
             recv_sem=red_sem.at[1], device_id=device, device_id_type=MESH,
         )
 
-    smooth()
-    e = correct()
-    value = jnp.where(row == 2, whole(tally(e)), known)
+    value = jnp.where(row == 2, whole(square * acc), known)
     part[...] = value
     red[me] = value
-    hear(2)
+    hear(1)
 
     if everyone <= 64:
         turn = jnp.where(2 * sfc >= n_sfc, 1, n_sfc - 1)
@@ -499,7 +505,8 @@
             return carry
 
         lax.fori_loop(1, everyone, go, 0)
-    for i, value in enumerate(finish(e, False)):
+    smooth()
+    for i, value in enumerate(owned(finish(correct(), mine, SUBS, rows - 2 * SUBS), SUBS)):
         w_ref[:, pl.ds(i * LANES, LANES)] = square * value
     settle(0)
 
@@ -546,7 +553,9 @@
             vmem((planes, width), f32),
             vmem((planes, width), f32),
             vmem((2 * LANES, 12 * LANES), jnp.bfloat16),
-            fine, fine, fine, fine, coarse, coarse, coarse,
+            fine, fine, fine, fine,
+            vmem((3 * tiles, rows, LANES), f32),
+            coarse, coarse, coarse,
             vmem((3, rows, LANES), f32),
             vmem((3, crows, LANES), f32),
             vmem((planes, LANES), f32),
@@ -560,7 +569,7 @@
             dma((2,)),
             dma((3,)),
             dma((2,)),
-            pltpu.SemaphoreType.REGULAR((3,)),
+            pltpu.SemaphoreType.REGULAR((2,)),
         ],
         compiler_params=pltpu.CompilerParams(
             collective_id=0, has_side_effects=True, vmem_limit_bytes=16 * 1024 * 1024

time: 20.5 us -> 19.8 us (0.966)
  Pallas kernels: 19.1 us -> 18.4 us
    pallas_call x1, Pallas kernels: 18.4 us -> 17.7 us  [shards(): pl.pallas_call(functools.partial(kernel, (slots, edge, tiles, n_sfc, n_gr...]
where the time goes in v4:
time: 19.8 us; the launch traced here: 19.7 us
  Pallas kernels  18.4 us (93%)
  between operations  1.28 us (6%)
    pallas_call x1, Pallas kernels, shards(): pl.pallas_call(functools.partial(kernel, (slots, edge, tiles, n_sfc, n_gr...  17.7 us
    pallas_call x1, Pallas kernels, shards(): pl.pallas_call(combine, out_shape=(out, out, out), in_specs=[pl.BlockSpec...  0.72 us

profile of v4, /device:TPU:0, one launch (start us, length us, event | category | flops | bytes accessed | tf_op | source)
XLA Modules:
  0.0 19.7 jit_solution(10501651331547958371)
XLA Ops:
  1.3 17.7 %pcg.1 = (f32[64,256]{1,0:T(8,128)S(1)}, f32[64,256]{1,0:T(8,128)S(1)}, f32[64,256]{1,0:T(8,128)S(1)}, f32[64,256]{1,0:T(8,128)S(1)}, f32[2,128]{1,0:T(2,128)S(1)}) custom-call(s32[1]{0:T(128)S(6)} %copy.6.count_hbm, f32[64,256]{1,0:T(8,128)} %bitcast.4, bf16[128,1536]{1,0:T(8,128)(2,1)} %constant.2.clone.weight_hbm), custom_call_target="tpu_custom_call" | custom-call | tf_op jit(solution)/shard_map/pcg/pallas_call | solution.py:547
  18.9 0.7 %combine.1 = (f32[64,256]{1,0:T(8,128)}, f32[64,256]{1,0:T(8,128)}, f32[64,256]{1,0:T(8,128)}) custom-call(f32[64,256]{1,0:T(8,128)S(1)} %get-tuple-element.11.first, f32[64,256]{1,0:T(8,128)S(1)} %get-tuple-element.12.image, f32[64,256]{1,0:T(8,128)S(1)} %get-tuple-element.13.w, f32[64,256]{1,0:T(8,128)S(1)} %get-tuple-element.14.source, ...), custom_call_target="tpu_custom_call" | custom-call | tf_op jit(solution)/shard_map/combine/pallas_call | solution.py:579

commit v5 on v4

--- a/solution.py
+++ b/solution.py
@@ -13,7 +13,7 @@
 SUBS = 8
 STEP = 1.0 / 9.0
 CSTEP = 4.0 / 9.0
-WAYS = ((0, 1), (0, -1), (1, 0), (1, 1), (1, -1), (-1, 0), (-1, 1), (-1, -1))
+WAYS = ((1, 1), (1, -1), (-1, 1), (-1, -1), (1, 0), (-1, 0), (0, 1), (0, -1))
 
 
 def weights(edge):
@@ -91,12 +91,6 @@
         pl.semaphore_signal(barrier, inc=1, device_id=place(i)[1], device_id_type=MESH)
         return carry
 
-    source_copy = pltpu.make_async_copy(source_hbm, source_ref, local_sem.at[0])
-    source_copy.start()
-    for up in (0, 1):
-        pltpu.make_async_copy(
-            weight_hbm, weight_ref.at[pl.ds(up * LANES, LANES), :], local_sem.at[1]
-        ).start()
     if gossip:
         for ds, dg in WAYS:
             @pl.when(there(ds, dg))
@@ -108,6 +102,12 @@
     else:
         lax.fori_loop(1, everyone, greet, 0)
 
+    source_copy = pltpu.make_async_copy(source_hbm, source_ref, local_sem.at[0])
+    source_copy.start()
+    for up in range(3):
+        pltpu.make_async_copy(
+            weight_hbm, weight_ref.at[pl.ds(up * LANES, LANES), :], local_sem.at[1]
+        ).start()
     def one(flag):
         return jnp.where(flag, 1, 0)
 
@@ -167,7 +167,7 @@
             target = (below if ds > 0 else above).at[e, gpos, pl.ds(0, amount)]
         return pltpu.make_async_remote_copy(
             src_ref=source, dst_ref=target, send_sem=trade_sem.at[0],
-            recv_sem=trade_sem.at[1 + e], device_id={"sfc": sfc + ds, "grp": grp + dg},
+            recv_sem=trade_sem.at[1 if e == 0 else 2 if (dg, ds) < (0, 0) else 3], device_id={"sfc": sfc + ds, "grp": grp + dg},
             device_id_type=MESH,
         )
 
@@ -177,21 +177,25 @@
             def _(ds=ds, dg=dg):
                 copies(e, ds, dg, src).start()
 
-    def settle(sem):
-        column = slots * edge * tiles // SUBS
-        for beside in range(3):
-            for along in range(3):
-                total = beside * column + along * (3 + 2 * beside)
-
-                @pl.when(
-                    jnp.logical_and(
-                        has_left + has_right == beside, has_below + has_above == along
-                    )
-                )
-                def _(total=total):
-                    if total:
-                        ref = dummy.at[pl.ds(0, total)]
-                        pltpu.make_async_copy(ref, ref, trade_sem.at[sem]).wait()
+    column = slots * edge * tiles // SUBS
+    ends, layers = has_left + has_right, has_below + has_above
+
+    def settle(sem, amounts, times=1):
+        for flags, tiles_in in amounts:
+            if tiles_in:
+                @pl.when(functools.reduce(jnp.logical_and, flags))
+                def _(tiles_in=tiles_in):
+                    ref = dummy.at[pl.ds(0, times * tiles_in)]
+                    pltpu.make_async_copy(ref, ref, trade_sem.at[sem]).wait()
+
+    def half_of(beside, along):
+        return [
+            ((beside == b, along == a, layers == l), b * (column + 2 * l) + 3 * a)
+            for b in (0, 1) for l in (0, 1, 2) for a in (0, 1) if l - 1 <= a <= l
+        ]
+
+    both = [((ends == b, layers == l), b * (column + 2 * l) + 3 * l) for b in range(3) for l in range(3)]
+    high, low_end = half_of(has_right, has_above), half_of(has_left, has_below)
 
     def pack(e, src):
         cut = SUBS // 2
@@ -276,11 +280,9 @@
     def product(values, pieces, at, width):
         n = values[0].shape[0]
         parts = [split(v, pieces) for v in values]
-        pair = jnp.concatenate([jnp.concatenate(p[:2], axis=1) for p in parts], axis=0)
-        out = jnp.dot(pair, weight_ref[:, pl.ds(at, width)], preferred_element_type=f32)
-        if pieces == 3:
-            last = jnp.concatenate([p[2] for p in parts], axis=0)
-            out = out + jnp.dot(last, weight_ref[pl.ds(0, LANES), pl.ds(at, width)], preferred_element_type=f32)
+        lhs = jnp.concatenate([jnp.concatenate(p, axis=1) for p in parts], axis=0)
+        w = weight_ref[pl.ds(0, pieces * LANES), pl.ds(at, width)]
+        out = jnp.dot(lhs, w, preferred_element_type=f32)
 
         def get(i, k):
             return out[i * n : (i + 1) * n, k * LANES : (k + 1) * LANES]
@@ -319,7 +321,8 @@
             first = get(t, 0) + blend(get, t, 1, wide, rows)
             seconds.append(walls(get(t, 2) + blend(get, t, 3, wide, rows), r, t))
             near = around(rhs, t)
-            pre[t, pl.ds(SUBS, rows), :] = 9.0 * r + near + 0.5 * first
+            if t in mids:
+                pre[t, pl.ds(SUBS, rows), :] = 9.0 * r + near + 0.5 * first
             gather[t, pl.ds(SUBS, rows), :] = mask[1] * (first + near)
         for t in range(wide):
             other[t, pl.ds(SUBS, rows), :] = seconds[t] + around(gather, t)
@@ -341,7 +344,12 @@
         left, right = mids[0], mids[-1]
         qs[left] = jnp.where(has(has_left), qs[left], reflect(qs[mine[0]], False))
         qs[right] = jnp.where(has(has_right), qs[right], reflect(qs[mine[-1]], True))
-        get = product(qs, 2, 4 * LANES, 8 * LANES)
+        powers = product([qs[t] for t in mids], 2, 4 * LANES, 4 * LANES)
+        sides = product(qs, 2, 8 * LANES, 4 * LANES)
+
+        def get(i, k):
+            return powers(i - mids[0], k) if k < 4 else sides(i, k - 4)
+
         b0, b1, b2 = {}, {}, {}
         for t in mids:
             c = get(t, 0)
@@ -384,20 +392,28 @@
             second = blend(get, i, 3, near, n)
             if t in mids:
                 second = walls(get(i, 2) + second, body(other, t, low, n), t)
-            out[t] = body(pre, t, low, n) + square * (second + around(gather, t, low, n))
+            out[t] = square * (second + around(gather, t, low, n))
+            if t in mids:
+                out[t] = body(pre, t, low, n) + out[t]
         return out
 
     def owned(out, low):
         return [own[...] * out[t][edge - low : edge - low + planes] for t in mine]
 
     def laplace():
-        get = product([body(gather, t, edge, planes) for t in mids], 3, 0, 2 * LANES)
+        lanes = lax.broadcasted_iota(jnp.int32, (planes, LANES), 1)
+        z = lanes % edge
+        tile = {t: body(gather, t, edge, planes) for t in mids}
+        ahead = {t: pltpu.roll(tile[t], LANES - edge, 1) for t in mids[1:]}
+        behind = {t: pltpu.roll(tile[t], edge, 1) for t in mids[:-1]}
         out = []
-        for i, t in enumerate(mids):
-            if t in mine:
-                first = get(i, 0) + blend(get, i, 1, len(mids), planes)
-                value = 9.0 * body(gather, t, edge, planes) - around(gather, t, edge, planes) - 0.5 * first
-                out.append(square * (own[...] * value))
+        for t in mine:
+            v = tile[t]
+            beside = jnp.where(z < edge - 1, pltpu.roll(v, LANES - 1, 1), 0.0)
+            beside = beside + jnp.where(z > 0, pltpu.roll(v, 1, 1), 0.0)
+            beside = beside + jnp.where(lanes < LANES - edge, ahead[t], ahead[t + 1])
+            beside = beside + jnp.where(lanes >= edge, behind[t], behind[t - 1])
+            out.append(square * (own[...] * (6.0 * v - around(gather, t, edge, planes) - beside)))
         return out
 
     count = count_hbm[0]
@@ -426,7 +442,7 @@
             own[pl.ds(s * edge + h * SUBS, SUBS), :] = value
     pltpu.make_async_copy(weight_ref, weight_ref, local_sem.at[1]).wait()
 
-    settle(1)
+    settle(1, both)
     tell(0)
     unpack(0, source_ref)
     smooth()
@@ -439,7 +455,6 @@
     for i, value in enumerate(images):
         image_buf[:, pl.ds(i * LANES, LANES)] = value
     pack(1, image_buf)
-    settle(0)
     start(1, image_buf)
     hear(0)
     tell(1)
@@ -473,11 +488,30 @@
     out = finish(correct(), range(wide), 0, rows)
     for t in range(wide):
         dual[t] = mask[spot(t)] * out[t]
-    settle(2)
-    unpack(1, image_buf)
     acc = zero
-    for t in range(wide):
-        acc = acc + jnp.sum((dual[t] * body(rhs, t)).reshape(-1, SUBS, LANES), axis=0)
+    for t in mine:
+        part_of = dual[t, pl.ds(edge, planes), :] * images[t - tiles]
+        acc = acc + jnp.sum(part_of.reshape(-1, SUBS, LANES), axis=0)
+    settle(2, high)
+    pairs = zero
+    for g, present in ((1, 1), (2, has_right)):
+        for s in range(slots + 2):
+            for h in range(edge // SUBS):
+                for t in range(tiles):
+                    if s == 0:
+                        value = jnp.where(has(has_below * present), ghost(below, 1, 1, g, h, t), 0.0)
+                    else:
+                        value = zero
+                        if s >= 2:
+                            up = one(count == s - 1) * has_above * present
+                            value = jnp.where(has(up), ghost(above, 1, 0, g, h, t), value)
+                        if g == 2 and s <= slots:
+                            at = pl.ds((s - 1) * edge + h * SUBS, SUBS)
+                            centre = side[1, 1, at, pl.ds(t * LANES, LANES)]
+                            value = jnp.where(has(one(count >= s) * present), centre, value)
+                    if g == 2 or s >= 2:
+                        pairs = pairs + dual[g * tiles + t, pl.ds(s * edge + h * SUBS, SUBS), :] * value
+    acc = acc + 2.0 * pairs
 
     def send(slot, device):
         return pltpu.make_async_remote_copy(
@@ -485,7 +519,7 @@
             recv_sem=red_sem.at[1], device_id=device, device_id_type=MESH,
         )
 
-    value = jnp.where(row == 2, whole(square * acc), known)
+    value = jnp.concatenate([square * jnp.sum(acc, axis=0, keepdims=True), known], axis=0)
     part[...] = value
     red[me] = value
     hear(1)
@@ -505,21 +539,25 @@
             return carry
 
         lax.fori_loop(1, everyone, go, 0)
+    settle(3, low_end)
+    unpack(1, image_buf)
     smooth()
     for i, value in enumerate(owned(finish(correct(), mine, SUBS, rows - 2 * SUBS), SUBS)):
         w_ref[:, pl.ds(i * LANES, LANES)] = square * value
-    settle(0)
+    settle(0, both, 2)
 
     rest = red.at[pl.ds(0, everyone - 1)]
     pltpu.make_async_copy(rest, rest, red_sem.at[0]).wait()
     pltpu.make_async_copy(rest, rest, red_sem.at[1]).wait()
     sums = jnp.sum(red[...], axis=0)
 
-    def pick(i):
-        return jnp.sum(jnp.where(row == i, sums, 0.0), axis=1, keepdims=True)
-
-    alpha = pick(0) / pick(1)
-    ratio = pick(2) / pick(1)
+    def pick(value):
+        return jnp.sum(value, axis=1, keepdims=True)
+
+    rz = pick(jnp.where(row == 0, sums[1:], 0.0))
+    inverse = 1.0 / pick(jnp.where(row == 1, sums[1:], 0.0))
+    alpha = rz * inverse
+    ratio = pick(sums[:1]) * inverse
     scale_ref[...] = jnp.concatenate(
         [jnp.broadcast_to(alpha, (1, LANES)), jnp.broadcast_to(ratio, (1, LANES))], axis=0
     )
@@ -552,7 +590,7 @@
         scratch_shapes=[
             vmem((planes, width), f32),
             vmem((planes, width), f32),
-            vmem((2 * LANES, 12 * LANES), jnp.bfloat16),
+            vmem((3 * LANES, 12 * LANES), jnp.bfloat16),
             fine, fine, fine, fine,
             vmem((3 * tiles, rows, LANES), f32),
             coarse, coarse, coarse,
@@ -563,11 +601,11 @@
             vmem((2, 2, planes, width), f32),
             vmem((2, 3, 3, SUBS, LANES), f32),
             vmem((2, 3, 3, SUBS, LANES), f32),
-            vmem((1, LANES), f32),
-            vmem((n, 1, LANES), f32),
-            vmem((2 * planes * tiles // SUBS + 14, SUBS, LANES), f32),
+            vmem((2, LANES), f32),
+            vmem((n, 2, LANES), f32),
+            vmem((4 * planes * tiles // SUBS + 28, SUBS, LANES), f32),
             dma((2,)),
-            dma((3,)),
+            dma((4,)),
             dma((2,)),
             pltpu.SemaphoreType.REGULAR((2,)),
         ],

time: 19.8 us -> 19.6 us (0.990)
  Pallas kernels: 18.4 us -> 18.2 us
where the time goes in v5:
time: 19.6 us; the launch traced here: 19.5 us
  Pallas kernels  18.2 us (93%)
  between operations  1.28 us (7%)
    pallas_call x1, Pallas kernels, shards(): pl.pallas_call(functools.partial(kernel, (slots, edge, tiles, n_sfc, n_gr...  17.5 us
    pallas_call x1, Pallas kernels, shards(): pl.pallas_call(combine, out_shape=(out, out, out), in_specs=[pl.BlockSpec...  0.72 us

profile of v5, /device:TPU:0, one launch (start us, length us, event | category | flops | bytes accessed | tf_op | source)
XLA Modules:
  0.0 19.5 jit_solution(10907944555291784348)
XLA Ops:
  1.3 17.5 %pcg.1 = (f32[64,256]{1,0:T(8,128)S(1)}, f32[64,256]{1,0:T(8,128)S(1)}, f32[64,256]{1,0:T(8,128)S(1)}, f32[64,256]{1,0:T(8,128)S(1)}, f32[2,128]{1,0:T(2,128)S(1)}) custom-call(s32[1]{0:T(128)S(6)} %copy.6.count_hbm, f32[64,256]{1,0:T(8,128)} %bitcast.4, bf16[128,1536]{1,0:T(8,128)(2,1)} %constant.2.clone.weight_hbm), custom_call_target="tpu_custom_call" | custom-call | tf_op jit(solution)/shard_map/pcg/pallas_call | solution.py:585
  18.7 0.7 %combine.1 = (f32[64,256]{1,0:T(8,128)}, f32[64,256]{1,0:T(8,128)}, f32[64,256]{1,0:T(8,128)}) custom-call(f32[64,256]{1,0:T(8,128)S(1)} %get-tuple-element.11.first, f32[64,256]{1,0:T(8,128)S(1)} %get-tuple-element.12.image, f32[64,256]{1,0:T(8,128)S(1)} %get-tuple-element.13.w, f32[64,256]{1,0:T(8,128)S(1)} %get-tuple-element.14.source, ...), custom_call_target="tpu_custom_call" | custom-call | tf_op jit(solution)/shard_map/combine/pallas_call | solution.py:617

commit v6 on v5

--- a/solution.py
+++ b/solution.py
@@ -525,13 +525,12 @@
     hear(1)
 
     if everyone <= 64:
-        turn = jnp.where(2 * sfc >= n_sfc, 1, n_sfc - 1)
-        grps = [lax.rem(grp + i, n_grp) for i in range(n_grp)]
-        for ds in (*range(1, n_sfc), 0):
-            there_sfc = lax.rem(sfc + ds * turn, n_sfc)
-            for dg in range(n_grp):
-                if ds or dg:
-                    send(me, {"sfc": there_sfc, "grp": grps[dg]}).start()
+        for i in range(n_sfc - 1):
+            other_sfc = i + one(i >= sfc)
+            for g in range(n_grp):
+                send(me, {"sfc": other_sfc, "grp": g}).start()
+        for i in range(n_grp - 1):
+            send(me, {"sfc": sfc, "grp": i + one(i >= grp)}).start()
     else:
         def go(i, carry):
             peer, device = place(i)
@@ -549,7 +548,10 @@
     rest = red.at[pl.ds(0, everyone - 1)]
     pltpu.make_async_copy(rest, rest, red_sem.at[0]).wait()
     pltpu.make_async_copy(rest, rest, red_sem.at[1]).wait()
-    sums = jnp.sum(red[...], axis=0)
+    sums = red[...]
+    while sums.shape[0] % 2 == 0:
+        sums = sums[: sums.shape[0] // 2] + sums[sums.shape[0] // 2 :]
+    sums = jnp.sum(sums, axis=0)
 
     def pick(value):
         return jnp.sum(value, axis=1, keepdims=True)

time: 19.6 us -> 19.5 us (level)
  no operation moved by 1% of the time
where the time goes in v6:
time: 19.5 us; the launch traced here: 19.4 us
  Pallas kernels  18.1 us (93%)
  between operations  1.28 us (7%)
    pallas_call x1, Pallas kernels, shards(): pl.pallas_call(functools.partial(kernel, (slots, edge, tiles, n_sfc, n_gr...  17.4 us
    pallas_call x1, Pallas kernels, shards(): pl.pallas_call(combine, out_shape=(out, out, out), in_specs=[pl.BlockSpec...  0.72 us

profile of v6, /device:TPU:0, one launch (start us, length us, event | category | flops | bytes accessed | tf_op | source)
XLA Modules:
  0.0 19.4 jit_solution(5350032158174786234)
XLA Ops:
  1.3 17.4 %pcg.1 = (f32[64,256]{1,0:T(8,128)S(1)}, f32[64,256]{1,0:T(8,128)S(1)}, f32[64,256]{1,0:T(8,128)S(1)}, f32[64,256]{1,0:T(8,128)S(1)}, f32[2,128]{1,0:T(2,128)S(1)}) custom-call(s32[1]{0:T(128)S(6)} %copy.6.count_hbm, f32[64,256]{1,0:T(8,128)} %bitcast.4, bf16[128,1536]{1,0:T(8,128)(2,1)} %constant.2.clone.weight_hbm), custom_call_target="tpu_custom_call" | custom-call | tf_op jit(solution)/shard_map/pcg/pallas_call | solution.py:587
  18.7 0.7 %combine.1 = (f32[64,256]{1,0:T(8,128)}, f32[64,256]{1,0:T(8,128)}, f32[64,256]{1,0:T(8,128)}) custom-call(f32[64,256]{1,0:T(8,128)S(1)} %get-tuple-element.11.first, f32[64,256]{1,0:T(8,128)S(1)} %get-tuple-element.12.image, f32[64,256]{1,0:T(8,128)S(1)} %get-tuple-element.13.w, f32[64,256]{1,0:T(8,128)S(1)} %get-tuple-element.14.source, ...), custom_call_target="tpu_custom_call" | custom-call | tf_op jit(solution)/shard_map/combine/pallas_call | solution.py:619

commit v7 on v6

--- a/solution.py
+++ b/solution.py
@@ -197,18 +197,19 @@
     both = [((ends == b, layers == l), b * (column + 2 * l) + 3 * l) for b in range(3) for l in range(3)]
     high, low_end = half_of(has_right, has_above), half_of(has_left, has_below)
 
-    def pack(e, src):
+    def pack(e, src, columns=None):
         cut = SUBS // 2
+
+        def layer(s, t):
+            if columns is None:
+                return src[pl.ds(s * edge, edge), pl.ds(t * LANES, LANES)]
+            return columns[t][s * edge : (s + 1) * edge]
+
         for up in (0, 1):
-            at = pl.ds(0, edge)
-            value = [src[at, pl.ds(t * LANES, LANES)] for t in range(tiles)]
+            value = [layer(0, t) for t in range(tiles)]
             if up:
                 for s in range(1, slots):
-                    at = pl.ds(s * edge, edge)
-                    value = [
-                        jnp.where(count > s, src[at, pl.ds(t * LANES, LANES)], value[t])
-                        for t in range(tiles)
-                    ]
+                    value = [jnp.where(count > s, layer(s, t), value[t]) for t in range(tiles)]
             if up:
                 near = [v[edge - SUBS :] for v in value]
                 far = [v[edge - SUBS - cut : edge - SUBS] for v in value]
@@ -443,9 +444,9 @@
     pltpu.make_async_copy(weight_ref, weight_ref, local_sem.at[1]).wait()
 
     settle(1, both)
-    tell(0)
     unpack(0, source_ref)
     smooth()
+    tell(0)
     low, n = SUBS, rows - 2 * SUBS
     out = finish(correct(), mids, low, n)
     for t in mids:
@@ -454,7 +455,7 @@
     images = laplace()
     for i, value in enumerate(images):
         image_buf[:, pl.ds(i * LANES, LANES)] = value
-    pack(1, image_buf)
+    pack(1, None, images)
     start(1, image_buf)
     hear(0)
     tell(1)

time: 19.5 us -> 19.6 us (level)
  no operation moved by 1% of the time
where the time goes in v7:
time: 19.6 us; the launch traced here: 19.5 us
  Pallas kernels  18.2 us (93%)
  between operations  1.28 us (7%)
    pallas_call x1, Pallas kernels, shards(): pl.pallas_call(functools.partial(kernel, (slots, edge, tiles, n_sfc, n_gr...  17.5 us
    pallas_call x1, Pallas kernels, shards(): pl.pallas_call(combine, out_shape=(out, out, out), in_specs=[pl.BlockSpec...  0.72 us

profile of v7, /device:TPU:0, one launch (start us, length us, event | category | flops | bytes accessed | tf_op | source)
XLA Modules:
  0.0 19.5 jit_solution(12733888845877387916)
XLA Ops:
  1.3 17.5 %pcg.1 = (f32[64,256]{1,0:T(8,128)S(1)}, f32[64,256]{1,0:T(8,128)S(1)}, f32[64,256]{1,0:T(8,128)S(1)}, f32[64,256]{1,0:T(8,128)S(1)}, f32[2,128]{1,0:T(2,128)S(1)}) custom-call(s32[1]{0:T(128)S(6)} %copy.6.count_hbm, f32[64,256]{1,0:T(8,128)} %bitcast.4, bf16[128,1536]{1,0:T(8,128)(2,1)} %constant.2.clone.weight_hbm), custom_call_target="tpu_custom_call" | custom-call | tf_op jit(solution)/shard_map/pcg/pallas_call | solution.py:588
  18.8 0.7 %combine.1 = (f32[64,256]{1,0:T(8,128)}, f32[64,256]{1,0:T(8,128)}, f32[64,256]{1,0:T(8,128)}) custom-call(f32[64,256]{1,0:T(8,128)S(1)} %get-tuple-element.11.first, f32[64,256]{1,0:T(8,128)S(1)} %get-tuple-element.12.image, f32[64,256]{1,0:T(8,128)S(1)} %get-tuple-element.13.w, f32[64,256]{1,0:T(8,128)S(1)} %get-tuple-element.14.source, ...), custom_call_target="tpu_custom_call" | custom-call | tf_op jit(solution)/shard_map/combine/pallas_call | solution.py:620
